TPU v7x, 8 devices: a whole 2x2x1 slice. The times are simulated.
8 devices in a mesh: dp: 1 (over z), tp: 8 (over y, x, core).
Axes of the slice: x: 2, y: 2, z: 1, core: 2. Of those that a mesh axis runs over, the one named last changes fastest.
Arguments:
- x_steps: bfloat16 [32, 64, 4096], P(None, 'dp')
- cur_len: int32 [64], P('dp')
- k_cache: bfloat16 [2, 64, 64, 16, 256], P(None, 'dp', None, 'tp')
- v_cache: bfloat16 [2, 64, 64, 16, 256], P(None, 'dp', None, 'tp')
- ln_gain: bfloat16 [2, 4096], replicated
- ln_bias: bfloat16 [2, 4096], replicated
- w_q: bfloat16 [2, 4096, 4096], P(None, None, 'tp')
- w_k: bfloat16 [2, 4096, 4096], P(None, None, 'tp')
- w_v: bfloat16 [2, 4096, 4096], P(None, None, 'tp')
- w_o: bfloat16 [2, 4096, 4096], P(None, 'tp')
- w_in: bfloat16 [2, 4096, 16384], P(None, None, 'tp')
- b_in: bfloat16 [2, 16384], P(None, 'tp')
- w_out: bfloat16 [2, 16384, 4096], P(None, 'tp')
- b_out: bfloat16 [2, 4096], replicated
Outputs:
- output 1: bfloat16 [32, 64, 4096], P(None, 'dp')
- output 2: bfloat16 [2, 64, 64, 16, 256], P(None, 'dp', None, 'tp')
- output 3: bfloat16 [2, 64, 64, 16, 256], P(None, 'dp', None, 'tp')
All inputs are finite; a program needn't handle non-finite values.
Results may differ from a plain program's by a relative error of at most 0.0162712.
Values are sent between devices in bfloat16 or wider.
A program may use at most 1 GiB of HBM per device.

v0:
```python
import jax
import jax.numpy as jnp
from jax import lax
from jax.sharding import PartitionSpec as P

ROT_DIM = 64
LN_EPS = 1e-5


def layer_norm(hidden, gain, bias):
    hid_f32 = hidden.astype(jnp.float32)
    row_mean = jnp.mean(hid_f32, axis=-1, keepdims=True)
    centered = hid_f32 - row_mean
    row_var = jnp.mean(centered * centered, axis=-1, keepdims=True)
    normed = centered * lax.rsqrt(row_var + LN_EPS)
    return (normed * gain.astype(jnp.float32) + bias.astype(jnp.float32)).astype(jnp.bfloat16)


def rotary_tables(positions):
    inv_freq = 1.0 / (10000.0 ** (jnp.arange(0, ROT_DIM, 2).astype(jnp.float32) / ROT_DIM))
    angles = positions.astype(jnp.float32)[:, None] * inv_freq[None, :]
    return jnp.cos(angles)[:, None, :], jnp.sin(angles)[:, None, :]


def apply_rotary(vectors, cos_tab, sin_tab):
    lead_shape = vectors.shape[:-1]
    pairs = vectors[..., :ROT_DIM].reshape(lead_shape + (ROT_DIM // 2, 2))
    even_part = pairs[..., 0]
    odd_part = pairs[..., 1]
    rotated = jnp.stack([even_part * cos_tab - odd_part * sin_tab, odd_part * cos_tab + even_part * sin_tab], axis=-1)
    return jnp.concatenate([rotated.reshape(lead_shape + (ROT_DIM,)), vectors[..., ROT_DIM:]], axis=-1)


def attend(query, k_layer, v_layer, visible):
    score_scale = k_layer.shape[-1] ** -0.5
    scores = jnp.einsum("bhe,bshe->bhs", query, k_layer, preferred_element_type=jnp.float32) * score_scale
    scores = jnp.where(visible, scores, -jnp.inf)
    exp_scores = jnp.exp(scores - jnp.max(scores, axis=-1, keepdims=True))
    attn_probs = (exp_scores / jnp.sum(exp_scores, axis=-1, keepdims=True)).astype(jnp.bfloat16)
    context = jnp.einsum("bhs,bshe->bhe", attn_probs, v_layer, preferred_element_type=jnp.float32)
    return context.astype(jnp.bfloat16)


def step_setup(cur_len, step_idx, cache_len):
    new_pos = cur_len + step_idx
    slot_ids = jnp.arange(cache_len)
    visible = (slot_ids[None, :] <= new_pos[:, None])[:, None, :]
    return new_pos, rotary_tables(new_pos), visible


def layer_update(normed, new_pos, rotary, visible, caches, layer_idx, weights):
    cos_tab, sin_tab = rotary
    k_cache, v_cache = caches
    q_weight, k_weight, v_weight, o_weight, in_weight, in_bias, out_weight = weights
    batch = normed.shape[0]
    n_heads = k_cache.shape[3]
    head_dim = k_cache.shape[4]
    head_shape = (batch, n_heads, head_dim)
    query = jnp.dot(normed, q_weight, preferred_element_type=jnp.float32).reshape(head_shape)
    key_new = jnp.dot(normed, k_weight, preferred_element_type=jnp.float32).reshape(head_shape)
    value_new = jnp.dot(normed, v_weight, preferred_element_type=jnp.float32).astype(jnp.bfloat16).reshape(head_shape)
    query = apply_rotary(query, cos_tab, sin_tab).astype(jnp.bfloat16)
    key_new = apply_rotary(key_new, cos_tab, sin_tab).astype(jnp.bfloat16)
    batch_rows = jnp.arange(batch)
    k_cache = k_cache.at[layer_idx, batch_rows, new_pos].set(key_new)
    v_cache = v_cache.at[layer_idx, batch_rows, new_pos].set(value_new)
    context = attend(query, k_cache[layer_idx], v_cache[layer_idx], visible).reshape(batch, n_heads * head_dim)
    pre_act = jnp.dot(normed, in_weight, preferred_element_type=jnp.float32) + in_bias.astype(jnp.float32)
    gelu_act = jax.nn.gelu(pre_act, approximate=True).astype(jnp.bfloat16)
    layer_part = jnp.dot(context, o_weight, preferred_element_type=jnp.float32) + jnp.dot(gelu_act, out_weight, preferred_element_type=jnp.float32)
    return layer_part, k_cache, v_cache


def decode_shard(x_steps, cur_len, k_cache, v_cache, ln_gain, ln_bias, w_q, w_k, w_v, w_o, w_in, b_in, w_out, b_out):
    n_layers = k_cache.shape[0]
    outputs = []
    for step_idx in range(x_steps.shape[0]):
        new_pos, rotary, visible = step_setup(cur_len, step_idx, k_cache.shape[2])
        hidden = x_steps[step_idx]
        for layer_idx in range(n_layers):
            normed = layer_norm(hidden, ln_gain[layer_idx], ln_bias[layer_idx])
            weights = (w_q[layer_idx], w_k[layer_idx], w_v[layer_idx], w_o[layer_idx], w_in[layer_idx], b_in[layer_idx], w_out[layer_idx])
            layer_part, k_cache, v_cache = layer_update(normed, new_pos, rotary, visible, (k_cache, v_cache), layer_idx, weights)
            layer_sum = lax.psum(layer_part.astype(jnp.bfloat16), "tp")
            hidden = (hidden.astype(jnp.float32) + layer_sum.astype(jnp.float32) + b_out[layer_idx].astype(jnp.float32)).astype(jnp.bfloat16)
        outputs.append(hidden)
    return jnp.stack(outputs), k_cache, v_cache


def solution(mesh):
    cache_spec = P(None, "dp", None, "tp", None)
    in_specs = (P(None, "dp", None), P("dp"), cache_spec, cache_spec, P(None, None), P(None, None),
                P(None, None, "tp"), P(None, None, "tp"), P(None, None, "tp"), P(None, "tp", None),
                P(None, None, "tp"), P(None, "tp"), P(None, "tp", None), P(None, None))
    out_specs = (P(None, "dp", None), cache_spec, cache_spec)
    return jax.shard_map(decode_shard, mesh=mesh, in_specs=in_specs, out_specs=out_specs, check_vma=False)
```

profile of v0, /device:TPU:0, one launch (start us, length us, event | category | flops | bytes accessed | tf_op | source)
XLA Modules:
  0.0 6559.9 jit_solution(12514129008455596639)
XLA Ops:
  1274.6 42.4 all-reduce.37.cloned.1.call-done
  1441.0 38.9 all-reduce.39.cloned.1.call-done
  1603.4 38.9 all-reduce.41.cloned.1.call-done
  1765.7 38.9 all-reduce.43.cloned.1.call-done
  1928.8 38.9 all-reduce.45.cloned.1.call-done
  2092.6 38.9 all-reduce.47.cloned.1.call-done
  2256.4 38.9 all-reduce.49.cloned.1.call-done
  2420.1 39.0 all-reduce.51.cloned.1.call-done
  2584.0 38.9 all-reduce.53.cloned.1.call-done
  2747.8 38.9 all-reduce.55.cloned.1.call-done
  2911.6 38.9 all-reduce.57.cloned.1.call-done
  3075.4 38.9 all-reduce.59.cloned.1.call-done
  3239.2 38.9 all-reduce.61.cloned.1.call-done
  3403.0 38.9 all-reduce.63.cloned.1.call-done
  3566.8 38.9 all-reduce.65.cloned.1.call-done
  3730.6 38.9 all-reduce.67.cloned.1.call-done
  3894.4 38.9 all-reduce.69.cloned.1.call-done
  4058.2 39.0 all-reduce.71.cloned.1.call-done
  4222.0 38.9 all-reduce.73.cloned.1.call-done
  4385.8 39.0 all-reduce.75.cloned.1.call-done
  4549.7 38.9 all-reduce.77.cloned.1.call-done
  4713.4 38.9 all-reduce.79.cloned.1.call-done
  4877.2 39.0 all-reduce.81.cloned.1.call-done
  5041.1 39.0 all-reduce.83.cloned.1.call-done
  5204.9 38.9 all-reduce.85.cloned.1.call-done
  5368.7 38.9 all-reduce.87.cloned.1.call-done
  5532.5 38.9 all-reduce.89.cloned.1.call-done
  5696.3 39.0 all-reduce.91.cloned.1.call-done
  5860.1 38.9 all-reduce.93.cloned.1.call-done
  6023.9 38.9 all-reduce.95.cloned.1.call-done
  6187.7 38.9 all-reduce.97.cloned.1.call-done
  6297.4 234.7 %all-reduce.99.cloned.1.call-done = (bf16[64,4096]{1,0:T(8,128)(2,1)}, bf16[64,4096]{1,0:T(8,128)(2,1)}, bf16[64,4096]{1,0:T(8,128)(2,1)}, bf16[64,4096]{1,0:T(8...) async-done(((bf16[64,4096]{1,0:T(8,128)(2,1)}, ...) | async-done | bytes 16777232 | tf_op jit(solution)/shard_map/psum | solution.py:84
  (3493 shorter events, 5083.6 us)
Async XLA Ops:
  7.2 1142.7 %all-reduce.35.cloned.1.call-start = ((), (), s32[]{:S(2)}) async-start(), calls=%async_computation | async-start | bytes 1048576 | tf_op jit(solution)/shard_map/psum | solution.py:84
  144.5 1172.5 %all-reduce.37.cloned.1.call-start = ((), (), s32[]{:S(2)}) async-start(), calls=%async_computation.1 | async-start | bytes 1048576 | tf_op jit(solution)/shard_map/psum | solution.py:84
  1270.7 209.3 %all-reduce.39.cloned.1.call-start = ((), (), s32[]{:S(2)}) async-start(), calls=%async_computation.2 | async-start | bytes 1048576 | tf_op jit(solution)/shard_map/psum | solution.py:84
  1599.5 205.1 %all-reduce.43.cloned.1.call-start = ((), (), s32[]{:S(2)}) async-start(), calls=%async_computation.4 | async-start | bytes 1048576 | tf_op jit(solution)/shard_map/psum | solution.py:84
  1761.8 205.9 %all-reduce.45.cloned.1.call-start = ((), (), s32[]{:S(2)}) async-start(), calls=%async_computation.5 | async-start | bytes 1048576 | tf_op jit(solution)/shard_map/psum | solution.py:84
  1924.9 206.6 %all-reduce.47.cloned.1.call-start = ((), (), s32[]{:S(2)}) async-start(), calls=%async_computation.6 | async-start | bytes 1048576 | tf_op jit(solution)/shard_map/psum | solution.py:84
  2088.7 206.6 %all-reduce.49.cloned.1.call-start = ((), (), s32[]{:S(2)}) async-start(), calls=%async_computation.7 | async-start | bytes 1048576 | tf_op jit(solution)/shard_map/psum | solution.py:84
  2252.5 206.6 %all-reduce.51.cloned.1.call-start = ((), (), s32[]{:S(2)}) async-start(), calls=%async_computation.8 | async-start | bytes 1048576 | tf_op jit(solution)/shard_map/psum | solution.py:84
  2416.3 206.6 %all-reduce.53.cloned.1.call-start = ((), (), s32[]{:S(2)}) async-start(), calls=%async_computation.9 | async-start | bytes 1048576 | tf_op jit(solution)/shard_map/psum | solution.py:84
  2580.1 206.6 %all-reduce.55.cloned.1.call-start = ((), (), s32[]{:S(2)}) async-start(), calls=%async_computation.10 | async-start | bytes 1048576 | tf_op jit(solution)/shard_map/psum | solution.py:84
  2743.9 206.6 %all-reduce.57.cloned.1.call-start = ((), (), s32[]{:S(2)}) async-start(), calls=%async_computation.11 | async-start | bytes 1048576 | tf_op jit(solution)/shard_map/psum | solution.py:84
  2907.7 206.6 %all-reduce.59.cloned.1.call-start = ((), (), s32[]{:S(2)}) async-start(), calls=%async_computation.12 | async-start | bytes 1048576 | tf_op jit(solution)/shard_map/psum | solution.py:84
  3071.5 206.6 %all-reduce.61.cloned.1.call-start = ((), (), s32[]{:S(2)}) async-start(), calls=%async_computation.13 | async-start | bytes 1048576 | tf_op jit(solution)/shard_map/psum | solution.py:84
  3235.3 206.6 %all-reduce.63.cloned.1.call-start = ((), (), s32[]{:S(2)}) async-start(), calls=%async_computation.14 | async-start | bytes 1048576 | tf_op jit(solution)/shard_map/psum | solution.py:84
  3399.1 206.6 %all-reduce.65.cloned.1.call-start = ((), (), s32[]{:S(2)}) async-start(), calls=%async_computation.15 | async-start | bytes 1048576 | tf_op jit(solution)/shard_map/psum | solution.py:84
  3562.9 206.6 %all-reduce.67.cloned.1.call-start = ((), (), s32[]{:S(2)}) async-start(), calls=%async_computation.16 | async-start | bytes 1048576 | tf_op jit(solution)/shard_map/psum | solution.py:84
  3726.7 206.6 %all-reduce.69.cloned.1.call-start = ((), (), s32[]{:S(2)}) async-start(), calls=%async_computation.17 | async-start | bytes 1048576 | tf_op jit(solution)/shard_map/psum | solution.py:84
  3890.5 206.6 %all-reduce.71.cloned.1.call-start = ((), (), s32[]{:S(2)}) async-start(), calls=%async_computation.18 | async-start | bytes 1048576 | tf_op jit(solution)/shard_map/psum | solution.py:84
  4054.3 206.6 %all-reduce.73.cloned.1.call-start = ((), (), s32[]{:S(2)}) async-start(), calls=%async_computation.19 | async-start | bytes 1048576 | tf_op jit(solution)/shard_map/psum | solution.py:84
  4218.1 206.6 %all-reduce.75.cloned.1.call-start = ((), (), s32[]{:S(2)}) async-start(), calls=%async_computation.20 | async-start | bytes 1048576 | tf_op jit(solution)/shard_map/psum | solution.py:84
  4382.0 206.6 %all-reduce.77.cloned.1.call-start = ((), (), s32[]{:S(2)}) async-start(), calls=%async_computation.21 | async-start | bytes 1048576 | tf_op jit(solution)/shard_map/psum | solution.py:84
  4545.8 206.6 %all-reduce.79.cloned.1.call-start = ((), (), s32[]{:S(2)}) async-start(), calls=%async_computation.22 | async-start | bytes 1048576 | tf_op jit(solution)/shard_map/psum | solution.py:84
  4709.6 206.6 %all-reduce.81.cloned.1.call-start = ((), (), s32[]{:S(2)}) async-start(), calls=%async_computation.23 | async-start | bytes 1048576 | tf_op jit(solution)/shard_map/psum | solution.py:84
  4873.4 206.6 %all-reduce.83.cloned.1.call-start = ((), (), s32[]{:S(2)}) async-start(), calls=%async_computation.24 | async-start | bytes 1048576 | tf_op jit(solution)/shard_map/psum | solution.py:84
  5037.2 206.6 %all-reduce.85.cloned.1.call-start = ((), (), s32[]{:S(2)}) async-start(), calls=%async_computation.25 | async-start | bytes 1048576 | tf_op jit(solution)/shard_map/psum | solution.py:84
  5201.0 206.6 %all-reduce.87.cloned.1.call-start = ((), (), s32[]{:S(2)}) async-start(), calls=%async_computation.26 | async-start | bytes 1048576 | tf_op jit(solution)/shard_map/psum | solution.py:84
  5364.8 206.6 %all-reduce.89.cloned.1.call-start = ((), (), s32[]{:S(2)}) async-start(), calls=%async_computation.27 | async-start | bytes 1048576 | tf_op jit(solution)/shard_map/psum | solution.py:84
  5528.6 206.6 %all-reduce.91.cloned.1.call-start = ((), (), s32[]{:S(2)}) async-start(), calls=%async_computation.28 | async-start | bytes 1048576 | tf_op jit(solution)/shard_map/psum | solution.py:84
  5692.4 206.6 %all-reduce.93.cloned.1.call-start = ((), (), s32[]{:S(2)}) async-start(), calls=%async_computation.29 | async-start | bytes 1048576 | tf_op jit(solution)/shard_map/psum | solution.py:84
  5856.2 206.6 %all-reduce.95.cloned.1.call-start = ((), (), s32[]{:S(2)}) async-start(), calls=%async_computation.30 | async-start | bytes 1048576 | tf_op jit(solution)/shard_map/psum | solution.py:84
  6020.0 206.6 %all-reduce.97.cloned.1.call-start = ((), (), s32[]{:S(2)}) async-start(), calls=%async_computation.31 | async-start | bytes 1048576 | tf_op jit(solution)/shard_map/psum | solution.py:84
  6183.8 348.2 %all-reduce.99.cloned.1.call-start = ((), (), s32[]{:S(2)}) async-start(), calls=%async_computation.32 | async-start | bytes 33554432 | tf_op jit(solution)/shard_map/psum | solution.py:84
  (687 other events, 17555.5 us)
Sparse Core Ops, SparseCore 0:
  144.6 46.1 all-reduce.34
  1270.8 46.1 all-reduce.36
  1437.3 42.6 all-reduce.38
  1599.6 42.6 all-reduce.40
  1761.9 42.6 all-reduce.42
  2088.8 42.6 all-reduce.46
  2252.6 42.6 all-reduce.48
  2416.4 42.6 all-reduce.50
  2580.2 42.6 all-reduce.52
  2744.0 42.6 all-reduce.54
  2907.8 42.6 all-reduce.56
  3071.6 42.6 all-reduce.58
  3235.4 42.6 all-reduce.60
  3399.2 42.6 all-reduce.62
  3563.0 42.6 all-reduce.64
  3726.8 42.6 all-reduce.66
  3890.7 42.6 all-reduce.68
  4054.5 42.6 all-reduce.70
  4218.3 42.6 all-reduce.72
  4382.1 42.6 all-reduce.74
  4545.9 42.6 all-reduce.76
  4709.7 42.6 all-reduce.78
  4873.5 42.6 all-reduce.80
  5037.3 42.6 all-reduce.82
  5201.1 42.6 all-reduce.84
  5364.9 42.6 all-reduce.86
  5528.7 42.6 all-reduce.88
  5692.5 42.6 all-reduce.90
  5856.3 42.6 all-reduce.92
  6020.1 42.6 all-reduce.94
  6183.9 42.6 all-reduce.96
  6297.5 234.4 all-reduce.98
  (1 shorter events, 42.6 us)
where the time goes:
time: 6600 us; the launch traced here: 6560 us
  local copies, waits for them, and re-layouts  2760 us (42%)
  matrix products  2020 us (31%)
  waiting for transfers between devices  1450 us (22%)
  other arithmetic  297 us (4%)
    psum x33, waiting for transfers between devices, decode_shard(): layer_sum = lax.psum(layer_part.astype(jnp.bfloat16), 'tp')  1450 us
    dot_general x64, matrix products, layer_update(): jnp.dot(gelu_act, out_weight, preferred_element_type=jnp.float32)  932 us
    squeeze x64, local copies, waits for them, and re-layouts, layer_update(): v_cache[layer_idx]  669 us
    squeeze x64, local copies, waits for them, and re-layouts, layer_update(): k_cache[layer_idx]  659 us
    scatter x64, local copies, waits for them, and re-layouts, layer_update(): v_cache = v_cache.at[layer_idx, batch_rows, new_pos].set(value_new)  599 us
    scatter x64, local copies, waits for them, and re-layouts, layer_update(): k_cache = k_cache.at[layer_idx, batch_rows, new_pos].set(key_new)  583 us
    dot_general x64, matrix products, layer_update(): jnp.dot(context, o_weight, preferred_element_type=jnp.float32)  245 us
    dot_general x64, matrix products, layer_update(): jnp.dot(normed, v_weight, preferred_element_type=jnp.float32)  245 us
  transfers between devices with their start and end apart: 33, of which 32 were waited for; matrix products, arithmetic and copies ran while one was open for 17% of the time, Pallas kernels for 0%

commit v1 on v0

v1 whole, which is shorter than its diff:
```python
import jax
import jax.numpy as jnp
from jax import lax
from jax.sharding import PartitionSpec as P

ROT_DIM = 64
LN_EPS = 1e-5
N_CHUNKS = 2


def layer_norm(hidden, gain, bias):
    hid_f32 = hidden.astype(jnp.float32)
    row_mean = jnp.mean(hid_f32, axis=-1, keepdims=True)
    centered = hid_f32 - row_mean
    row_var = jnp.mean(centered * centered, axis=-1, keepdims=True)
    normed = centered * lax.rsqrt(row_var + LN_EPS)
    return (normed * gain.astype(jnp.float32) + bias.astype(jnp.float32)).astype(jnp.bfloat16)


def apply_rotary(vec, cos_tab, sin_tab):
    lead = vec.shape[:-1]
    pairs = vec[..., :ROT_DIM].reshape(lead + (ROT_DIM // 2, 2))
    even, odd = pairs[..., 0], pairs[..., 1]
    rot = jnp.stack([even * cos_tab - odd * sin_tab, odd * cos_tab + even * sin_tab], axis=-1)
    return jnp.concatenate([rot.reshape(lead + (ROT_DIM,)), vec[..., ROT_DIM:]], axis=-1)


def layer_part(normed, cur_len, k_old, v_old, weights):
    w_q, w_k, w_v, w_o, w_in, b_in, w_out = weights
    batch, slots, heads, dim = k_old.shape
    steps = normed.shape[0] // batch
    pos = cur_len[None, :] + jnp.arange(steps)[:, None]
    inv_freq = 1.0 / (10000.0 ** (jnp.arange(0, ROT_DIM, 2).astype(jnp.float32) / ROT_DIM))
    angles = pos.astype(jnp.float32)[..., None] * inv_freq
    cos_tab, sin_tab = jnp.cos(angles)[:, :, None, :], jnp.sin(angles)[:, :, None, :]
    shape = (steps, batch, heads, dim)
    query = jnp.dot(normed, w_q, preferred_element_type=jnp.float32).reshape(shape)
    key = jnp.dot(normed, w_k, preferred_element_type=jnp.float32).reshape(shape)
    value = jnp.dot(normed, w_v, preferred_element_type=jnp.float32).astype(jnp.bfloat16).reshape(shape)
    query = apply_rotary(query, cos_tab, sin_tab).astype(jnp.bfloat16)
    key = apply_rotary(key, cos_tab, sin_tab).astype(jnp.bfloat16)
    slot_ids = jnp.arange(slots)
    onehot = (slot_ids[None, :, None] == pos.T[:, None, :]).astype(jnp.bfloat16)
    written = jnp.any(onehot > 0, axis=-1)[:, :, None, None]
    k_all = jnp.where(written, jnp.einsum("bst,tbhe->bshe", onehot, key), k_old)
    v_all = jnp.where(written, jnp.einsum("bst,tbhe->bshe", onehot, value), v_old)
    scores = jnp.einsum("tbhe,bshe->bhts", query, k_all, preferred_element_type=jnp.float32) * (dim ** -0.5)
    visible = slot_ids[None, None, :] <= pos.T[:, :, None]
    scores = jnp.where(visible[:, None], scores, -jnp.inf)
    exps = jnp.exp(scores - jnp.max(scores, axis=-1, keepdims=True))
    probs = (exps / jnp.sum(exps, axis=-1, keepdims=True)).astype(jnp.bfloat16)
    context = jnp.einsum("bhts,bshe->tbhe", probs, v_all, preferred_element_type=jnp.float32).astype(jnp.bfloat16)
    context = context.reshape(steps * batch, heads * dim)
    pre_act = jnp.dot(normed, w_in, preferred_element_type=jnp.float32) + b_in.astype(jnp.float32)
    act = jax.nn.gelu(pre_act, approximate=True).astype(jnp.bfloat16)
    part = jnp.dot(context, w_o, preferred_element_type=jnp.float32) + jnp.dot(act, w_out, preferred_element_type=jnp.float32)
    return part.astype(jnp.bfloat16), k_all, v_all


def decode_shard(x_steps, cur_len, k_cache, v_cache, ln_gain, ln_bias, w_q, w_k, w_v, w_o, w_in, b_in, w_out, b_out):
    n_layers = k_cache.shape[0]
    steps, batch, width = x_steps.shape
    n_dev = lax.axis_size("tp")
    me = lax.axis_index("tp")
    group = batch // N_CHUNKS
    hiddens, normeds, outs = [], [], []
    k_new = [[None] * N_CHUNKS for _ in range(n_layers)]
    v_new = [[None] * N_CHUNKS for _ in range(n_layers)]
    own_rows = steps * group // n_dev
    for c in range(N_CHUNKS):
        rows = x_steps[:, c * group:(c + 1) * group].reshape(steps * group, width)
        hiddens.append(lax.dynamic_slice_in_dim(rows, me * own_rows, own_rows, 0))
        normeds.append(layer_norm(rows, ln_gain[0], ln_bias[0]))
    for layer in range(n_layers):
        weights = (w_q[layer], w_k[layer], w_v[layer], w_o[layer], w_in[layer], b_in[layer], w_out[layer])
        for c in range(N_CHUNKS):
            seqs = slice(c * group, (c + 1) * group)
            part, k_new[layer][c], v_new[layer][c] = layer_part(normeds[c], cur_len[seqs], k_cache[layer, seqs], v_cache[layer, seqs], weights)
            total = lax.psum_scatter(part, "tp", scatter_dimension=0, tiled=True)
            hiddens[c] = (hiddens[c].astype(jnp.float32) + total.astype(jnp.float32) + b_out[layer].astype(jnp.float32)).astype(jnp.bfloat16)
            if layer + 1 < n_layers:
                send = layer_norm(hiddens[c], ln_gain[layer + 1], ln_bias[layer + 1])
            else:
                send = hiddens[c]
            normeds[c] = lax.all_gather(send, "tp", axis=0, tiled=True)
    hidden_out = jnp.concatenate([n.reshape(steps, group, width) for n in normeds], axis=1)
    k_out = jnp.stack([jnp.concatenate(ks, axis=0) for ks in k_new])
    v_out = jnp.stack([jnp.concatenate(vs, axis=0) for vs in v_new])
    return hidden_out, k_out, v_out


def solution(mesh):
    cache_spec = P(None, "dp", None, "tp", None)
    in_specs = (P(None, "dp", None), P("dp"), cache_spec, cache_spec, P(None, None), P(None, None),
                P(None, None, "tp"), P(None, None, "tp"), P(None, None, "tp"), P(None, "tp", None),
                P(None, None, "tp"), P(None, "tp"), P(None, "tp", None), P(None, None))
    out_specs = (P(None, "dp", None), cache_spec, cache_spec)
    return jax.shard_map(decode_shard, mesh=mesh, in_specs=in_specs, out_specs=out_specs, check_vma=False)
```

time: 6600 us -> 951 us (0.14)
  local copies, waits for them, and re-layouts: 2760 us -> 198 us
  matrix products: 2020 us -> 363 us
  waiting for transfers between devices: 1450 us -> 231 us
  other arithmetic: 297 us -> 132 us
    dot_general x448 -> x40, matrix products: 2020 us -> 363 us  [the longest x4 104 us: layer_part(): jnp.dot(act, w_out, preferred_element_type=jnp.float32)]
    psum x33 -> x0, waiting for transfers between devices: 1450 us -> none  [decode_shard(): layer_sum = lax.psum(layer_part.astype(jnp.bfloat16), 'tp')]
    squeeze x128 -> x0, local copies, waits for them, and re-layouts: 1330 us -> none  [the longest x64 669 us: layer_update(): v_cache[layer_idx]]
    scatter x128 -> x0, local copies, waits for them, and re-layouts: 1180 us -> none  [the longest x64 599 us: layer_update(): v_cache = v_cache.at[layer_idx, batch_rows, new_pos].set(value_new)]
    all_gather x0 -> x4, waiting for transfers between devices: none -> 116 us  [decode_shard(): normeds[c] = lax.all_gather(send, 'tp', axis=0, tiled=True)]
    reduce_scatter x0 -> x4, waiting for transfers between devices: none -> 114 us  [decode_shard(): total = lax.psum_scatter(part, 'tp', scatter_dimension=0, tiled=True)]
  transfers between devices with their start and end apart: 33 -> 8, of which waited for: 32 -> 5; matrix products, arithmetic and copies ran while one was open for 17% -> 34% of each run, Pallas kernels for 0% -> 0%
where the time goes in v1:
time: 951 us; the launch traced here: 940 us
  matrix products  363 us (38%)
  waiting for transfers between devices  231 us (24%)
  local copies, waits for them, and re-layouts  198 us (21%)
  other arithmetic  132 us (14%)
  between operations  15.8 us (2%)
    all_gather x4, waiting for transfers between devices, decode_shard(): normeds[c] = lax.all_gather(send, 'tp', axis=0, tiled=True)  116 us
    reduce_scatter x4, waiting for transfers between devices, decode_shard(): total = lax.psum_scatter(part, 'tp', scatter_dimension=0, tiled=True)  114 us
    dot_general x4, matrix products, layer_part(): jnp.dot(act, w_out, preferred_element_type=jnp.float32)  104 us
    dot_general x4, matrix products, layer_part(): jnp.dot(normed, w_in, preferred_element_type=jnp.float32)  85.9 us
    dot_general x4, matrix products, layer_part(): jnp.dot(context, w_o, preferred_element_type=jnp.float32)  46.7 us
    unnamed x182, local copies, waits for them, and re-layouts  45 us
    slice x19, local copies, waits for them, and re-layouts, apply_rotary(): pairs = vec[..., :ROT_DIM].reshape(lead + (ROT_DIM // 2, 2))  32.3 us
    dot_general x4, matrix products, layer_part(): jnp.dot(normed, w_k, preferred_element_type=jnp.float32).reshape(shape)  32.1 us
  transfers between devices with their start and end apart: 8, of which 5 were waited for; matrix products, arithmetic and copies ran while one was open for 34% of the time, Pallas kernels for 0%

profile of v1, /device:TPU:0, one launch (start us, length us, event | category | flops | bytes accessed | tf_op | source)
XLA Modules:
  0.0 939.9 jit_solution(14249478859203161986)
XLA Ops:
  13.9 8.0 fusion.12
  40.4 14.0 %fusion.15 = (bf16[32,32,4096]{2,1,0:T(8,128)(2,1)}, bf16[32,32,4096]{2,1,0:T(8,128)(2,1)S(1)}) fusion(f32[4096]{0:T(1024)S(1)} %bitcast.295, f32[4096]{0:T(1024)S(1)} %bitcast.294, f32[32,32]{1,0:T(8,128)S(1)} %get-tuple-element.81, f32[32,32]{1,0:T(8,128)S(1)} %broadcast_multiply_fusion.1, bf16[32,64,4096]{2,1,0:T(8,128)(2,1)} %param.14, ...), kind=kLoop, calls=%fused_computation.19 | loop fusion | flops 50331648 | bytes 33603584 | tf_op jit(solution)/shard_map/convert_element_type | solution.py:17
  70.7 8.4 fusion.74
  82.2 13.1 %fusion.233 = (bf16[1,32,64,2,256]{4,3,2,1,0:T(2,128)(2,1)}, bf16[1,32,64,2,256]{4,3,2,1,0:T(2,128)(2,1)}, bf16[1,32,64,2,256]{4,3,2,1,0:T(2,128)(2,1)}, bf16[1,32,64,2,256]{4,3,2,1,0:T(2,128)(2,1)}) fusion(bf16[2,64,64,2,256]{4,3,2,1,0:T(2,128)(2,1)} %param.16), kind=kLoop, calls=%fused_computation.335 | loop fusion | bytes 16777216 | tf_op jit(solution)/shard_map/slice | solution.py:78
  95.4 7.9 fusion.234
  151.9 21.4 %fusion.28 = f32[1024,2048]{1,0:T(8,128)S(1)} fusion(bf16[1024,4096]{1,0:T(8,128)(2,1)} %bitcast.252, bf16[2,4096,2048]{2,1,0:T(8,128)(2,1)} %param.24), kind=kOutput, calls=%fused_computation.33 | convolution fusion | flops 17179869184 | bytes 33554432 | tf_op jit(solution)/shard_map/dot_general | solution.py:54
  173.4 25.9 %fusion.24 = f32[1024,4096]{1,0:T(8,128)} fusion(bf16[2,2048,4096]{2,1,0:T(8,128)(2,1)} %param.26, f32[1024,2048]{1,0:T(8,128)S(1)} %fusion.28, f32[2048]{0:T(1024)S(1)} %bitcast.302), kind=kOutput, calls=%fused_computation.29 | convolution fusion | flops 17200840704 | bytes 41951232 | tf_op jit(solution)/shard_map/dot_general | solution.py:56
  199.2 11.8 %add_convert_fusion.1 = bf16[1024,4096]{1,0:T(8,128)(2,1)} fusion(f32[1024,4096]{1,0:T(8,128)} %fusion.24, bf16[1024,512]{1,0:T(8,128)(2,1)S(1)} %bitcast.293, bf16[2,512,4096]{2,1,0:T(8,128)(2,1)} %param.23), kind=kOutput, calls=%fused_computation.38 | convolution fusion | flops 4303355904 | bytes 30408704 | tf_op jit(solution)/shard_map/dot_general | solution.py:56
  211.1 8.4 fusion.76
  222.0 7.1 fusion.78
  276.9 21.4 %fusion.30 = f32[1024,2048]{1,0:T(8,128)S(1)} fusion(bf16[1024,4096]{1,0:T(8,128)(2,1)} %bitcast.248, bf16[2,4096,2048]{2,1,0:T(8,128)(2,1)} %param.24), kind=kOutput, calls=%fused_computation.35 | convolution fusion | flops 17179869184 | bytes 33554432 | tf_op jit(solution)/shard_map/dot_general | solution.py:54
  298.3 25.9 %fusion.26 = f32[1024,4096]{1,0:T(8,128)} fusion(bf16[2,2048,4096]{2,1,0:T(8,128)(2,1)} %param.26, f32[1024,2048]{1,0:T(8,128)S(1)} %fusion.30, f32[2048]{0:T(1024)S(1)} %bitcast.303), kind=kOutput, calls=%fused_computation.31 | convolution fusion | flops 17200840704 | bytes 41951232 | tf_op jit(solution)/shard_map/dot_general | solution.py:56
  324.2 11.8 %add_convert_fusion.3 = bf16[1024,4096]{1,0:T(8,128)(2,1)} fusion(f32[1024,4096]{1,0:T(8,128)} %fusion.26, bf16[1024,512]{1,0:T(8,128)(2,1)S(1)} %bitcast.291, bf16[2,512,4096]{2,1,0:T(8,128)(2,1)} %param.23), kind=kOutput, calls=%fused_computation.40 | convolution fusion | flops 4303355904 | bytes 30408704 | tf_op jit(solution)/shard_map/dot_general | solution.py:56
  337.3 11.8 %fusion.232 = (bf16[32,32,4096]{2,1,0:T(8,128)(2,1)}, bf16[32,32,4096]{2,1,0:T(8,128)(2,1)}) fusion(bf16[32,64,4096]{2,1,0:T(8,128)(2,1)} %param.14), kind=kLoop, calls=%fused_computation.334 | loop fusion | bytes 33554432 | tf_op jit(solution)/shard_map/slice | solution.py:71
  349.1 52.1 %reduce-scatter.5.cloned.1.call-done = bf16[128,4096]{1,0:T(8,128)(2,1)} async-done(((bf16[1024,4096]{1,0:T(8,128)(2,1)}), bf16[128,4096]{1,0:T(8,128)(2,1)}) %reduce-scatter.5.cloned.1.call-update) | async-done | bytes 1048592 | tf_op jit(solution)/shard_map/reduce_scatter | solution.py:79
  420.9 35.2 %all-gather.5.cloned.1.call-done = bf16[1024,4096]{1,0:T(8,128)(2,1)} async-done(((bf16[128,4096]{1,0:T(8,128)(2,1)}), bf16[1024,4096]{1,0:T(8,128)(2,1)}) %all-gather.5.cloned.1.call-update) | async-done | bytes 8388624 | tf_op jit(solution)/shard_map/all_gather | solution.py:85
  456.2 8.6 fusion.241
  466.5 39.7 %all-gather.9.cloned.1.call-done = bf16[1024,4096]{1,0:T(8,128)(2,1)} async-done(((bf16[128,4096]{1,0:T(8,128)(2,1)}), bf16[1024,4096]{1,0:T(8,128)(2,1)}) %all-gather.9.cloned.1.call-update) | async-done | bytes 8388624 | tf_op jit(solution)/shard_map/all_gather | solution.py:85
  506.2 10.6 %fusion.243 = f32[32,32,2,256]{3,1,2,0:T(8,128)} fusion(bf16[32,32,4096,1]{2,1,3,0:T(8,128)(2,1)} %bitcast.310, bf16[2,256,4096,1]{2,1,0,3:T(8,128)(2,1)} %bitcast.277), kind=kOutput, calls=%fused_computation.345 | convolution fusion | flops 4294967296 | bytes 14680064 | tf_op jit(solution)/shard_map/dot_general | solution.py:38
  588.8 21.4 %fusion.22 = f32[1024,2048]{1,0:T(8,128)S(1)} fusion(bf16[1024,4096]{1,0:T(8,128)(2,1)} %all-gather.5.cloned.1.call-done, bf16[2,4096,2048]{2,1,0:T(8,128)(2,1)} %param.24), kind=kOutput, calls=%fused_computation.27 | convolution fusion | flops 17179869184 | bytes 33554432 | tf_op jit(solution)/shard_map/dot_general | solution.py:54
  610.3 26.3 %fusion.18 = f32[1024,4096]{1,0:T(8,128)} fusion(bf16[2,2048,4096]{2,1,0:T(8,128)(2,1)} %param.26, f32[1024,2048]{1,0:T(8,128)S(1)} %fusion.22, f32[2048]{0:T(1024)S(1)} %bitcast.300), kind=kOutput, calls=%fused_computation.23 | convolution fusion | flops 17200840704 | bytes 41951232 | tf_op jit(solution)/shard_map/dot_general | solution.py:56
  636.5 11.6 %add_convert_fusion.2 = bf16[1024,4096]{1,0:T(8,128)(2,1)} fusion(f32[1024,4096]{1,0:T(8,128)} %fusion.18, bf16[1024,512]{1,0:T(8,128)(2,1)S(1)} %bitcast.290, bf16[2,512,4096]{2,1,0:T(8,128)(2,1)} %param.23), kind=kOutput, calls=%fused_computation.39 | convolution fusion | flops 4303355904 | bytes 30408704 | tf_op jit(solution)/shard_map/dot_general | solution.py:56
  648.2 10.2 %fusion.157 = bf16[1024,512]{1,0:T(8,128)(2,1)} fusion(bf16[1024,4096]{1,0:T(8,128)(2,1)} %all-gather.9.cloned.1.call-done, bf16[2,4096,512]{2,1,0:T(8,128)(2,1)} %param.22), kind=kOutput, calls=%fused_computation.194 | convolution fusion | flops 4295491584 | bytes 13631488 | tf_op jit(solution)/shard_map/dot_general | solution.py:39
  694.5 21.6 %fusion.20 = f32[1024,2048]{1,0:T(8,128)S(1)} fusion(bf16[1024,4096]{1,0:T(8,128)(2,1)} %all-gather.9.cloned.1.call-done, bf16[2,4096,2048]{2,1,0:T(8,128)(2,1)} %param.24), kind=kOutput, calls=%fused_computation.25 | convolution fusion | flops 17179869184 | bytes 33554432 | tf_op jit(solution)/shard_map/dot_general | solution.py:54
  716.1 25.9 %fusion.16 = f32[1024,4096]{1,0:T(8,128)} fusion(bf16[2,2048,4096]{2,1,0:T(8,128)(2,1)} %param.26, f32[1024,2048]{1,0:T(8,128)S(1)} %fusion.20, f32[2048]{0:T(1024)S(1)} %bitcast.301), kind=kOutput, calls=%fused_computation.21 | convolution fusion | flops 17200840704 | bytes 41951232 | tf_op jit(solution)/shard_map/dot_general | solution.py:56
  742.0 11.6 %add_convert_fusion = bf16[1024,4096]{1,0:T(8,128)(2,1)} fusion(f32[1024,4096]{1,0:T(8,128)} %fusion.16, bf16[1024,512]{1,0:T(8,128)(2,1)S(1)} %bitcast.292, bf16[2,512,4096]{2,1,0:T(8,128)(2,1)} %param.23), kind=kOutput, calls=%fused_computation.37 | convolution fusion | flops 4303355904 | bytes 30408704 | tf_op jit(solution)/shard_map/dot_general | solution.py:56
  753.7 62.3 %reduce-scatter.11.cloned.1.call-done = bf16[128,4096]{1,0:T(8,128)(2,1)} async-done(((bf16[1024,4096]{1,0:T(8,128)(2,1)}), bf16[128,4096]{1,0:T(8,128)(2,1)}) %reduce-scatter.11.cloned.1.call-update) | async-done | bytes 1048592 | tf_op jit(solution)/shard_map/reduce_scatter | solution.py:79
  828.8 7.6 pad_maximum_fusion.1
  836.4 16.5 %copy.87 = bf16[2,64,64,2,256]{4,3,2,1,0:T(2,128)(2,1)} copy(bf16[2,64,64,2,256]{4,2,3,1,0:T(8,128)(2,1)} %pad_maximum_fusion.1) | data formatting | bytes 16777216
  861.6 16.3 %copy.88 = bf16[2,64,64,2,256]{4,3,2,1,0:T(2,128)(2,1)} copy(bf16[2,64,64,2,256]{4,2,3,1,0:T(8,128)(2,1)} %pad_maximum_fusion.2) | data formatting | bytes 16777216
  877.9 40.8 %all-gather.11.cloned.1.call-done = bf16[1024,4096]{1,0:T(8,128)(2,1)} async-done(((bf16[128,4096]{1,0:T(8,128)(2,1)}), bf16[1024,4096]{1,0:T(8,128)(2,1)}) %all-gather.11.cloned.1.call-update) | async-done | bytes 8388624 | tf_op jit(solution)/shard_map/all_gather | solution.py:85
  918.7 13.9 %pad_maximum_fusion = bf16[32,64,4096]{2,1,0:T(8,128)(2,1)} fusion(bf16[32,32,4096]{2,1,0:T(8,128)(2,1)} %bitcast.269, bf16[32,32,4096]{2,1,0:T(8,128)(2,1)} %bitcast.268), kind=kLoop, calls=%fused_computation.20 | loop fusion | flops 33554432 | bytes 33554432 | tf_op jit(solution)/shard_map/concatenate | solution.py:86
  (333 shorter events, 295.1 us)
Async XLA Ops:
  7.2 342.0 %reduce-scatter.9.cloned.1.call-start = ((), (), s32[]{:S(2)}) async-start(), calls=%async_computation.8 | async-start | bytes 9437184 | tf_op jit(solution)/shard_map/reduce_scatter | solution.py:79
  8.7 134.0 %copy-start.55 = (s32[32,32]{1,0:T(8,128)}, s32[32,32]{1,0:T(8,128)S(1)}, u32[]{:S(2)}) copy-start(s32[32,32]{1,0:T(8,128)S(1)} %get-tuple-element.80) | copy-start | bytes 12292
  8.9 133.7 %copy-start.59 = (pred[32,64]{1,0:T(8,128)(4,1)}, pred[32,64]{1,0:T(8,128)(4,1)S(1)}, u32[]{:S(2)}) copy-start(pred[32,64]{1,0:T(8,128)(4,1)S(1)} %compare_reduce_fusion) | copy-start | bytes 6148
  9.2 130.5 %copy-start.50 = (pred[32,32,64]{2,1,0:T(8,128)(4,1)}, pred[32,32,64]{2,1,0:T(8,128)(4,1)S(1)}, u32[]{:S(2)}) copy-start(pred[32,32,64]{2,1,0:T(8,128)(4,1)S(1)} %iota_compare_fusion) | copy-start | bytes 196612
  40.4 20.2 %slice-start.4 = ((s8[8388608]{0:T(1024)(128)(4,1)}), s8[4194304]{0:T(1024)(128)(4,1)S(1)}, s32[]{:S(2)}) async-start(s8[8388608]{0:T(1024)(128)(4,1)} %bitcast.264), calls=%async_computation.16 | async-start | bytes 8388608
  82.2 21.1 %slice-start.2 = ((s8[8388608]{0:T(1024)(128)(4,1)}), s8[4194304]{0:T(1024)(128)(4,1)S(1)}, s32[]{:S(2)}) async-start(s8[8388608]{0:T(1024)(128)(4,1)} %bitcast.253), calls=%async_computation.14 | async-start | bytes 8388608
  82.2 21.1 %slice-start.11 = ((s8[8388608]{0:T(1024)(128)(4,1)}), s8[4194304]{0:T(1024)(128)(4,1)S(1)}, s32[]{:S(2)}) async-start(s8[8388608]{0:T(1024)(128)(4,1)} %bitcast.304), calls=%async_computation.23 | async-start | bytes 8388608
  144.7 28.6 %copy-start.13 = (bf16[32,64,2,256]{3,1,2,0:T(8,128)(2,1)}, bf16[32,64,2,256]{3,1,2,0:T(8,128)(2,1)S(1)}, u32[]{:S(2)}) copy-start(bf16[32,64,2,256]{3,1,2,0:T(8,128)(2,1)S(1)} %fusion.142) | copy-start | bytes 6291460
  211.0 190.2 %reduce-scatter.5.cloned.1.call-start = ((), (), s32[]{:S(2)}) async-start(), calls=%async_computation.4 | async-start | bytes 9437184 | tf_op jit(solution)/shard_map/reduce_scatter | solution.py:79
  211.1 20.6 %slice-start = ((s8[8388608]{0:T(1024)(128)(4,1)}), s8[4194304]{0:T(1024)(128)(4,1)S(1)}, s32[]{:S(2)}) async-start(s8[8388608]{0:T(1024)(128)(4,1)} %bitcast.249), calls=%async_computation.12 | async-start | bytes 8388608
  211.1 20.6 %slice-start.13 = ((s8[8388608]{0:T(1024)(128)(4,1)}), s8[4194304]{0:T(1024)(128)(4,1)S(1)}, s32[]{:S(2)}) async-start(s8[8388608]{0:T(1024)(128)(4,1)} %bitcast.306), calls=%async_computation.25 | async-start | bytes 8388608
  269.7 28.6 %copy-start.15 = (bf16[32,64,2,256]{3,1,2,0:T(8,128)(2,1)}, bf16[32,64,2,256]{3,1,2,0:T(8,128)(2,1)S(1)}, u32[]{:S(2)}) copy-start(bf16[32,64,2,256]{3,1,2,0:T(8,128)(2,1)S(1)} %fusion.146) | copy-start | bytes 6291460
  336.0 120.2 %all-gather.5.cloned.1.call-start = ((), (), s32[]{:S(2)}) async-start(), calls=%async_computation.5 | async-start | bytes 9437184 | tf_op jit(solution)/shard_map/all_gather | solution.py:85
  349.1 56.2 %copy-start.63 = (f32[1,4096]{1,0:T(1,128)S(1)}, f32[1,4096]{1,0:T(1,128)}, u32[]{:S(2)}) copy-start(f32[1,4096]{1,0:T(1,128)} %get-tuple-element.67) | copy-start | bytes 49156
  349.1 56.2 %copy-start.64 = (f32[1,4096]{1,0:T(1,128)S(1)}, f32[1,4096]{1,0:T(1,128)}, u32[]{:S(2)}) copy-start(f32[1,4096]{1,0:T(1,128)} %get-tuple-element.69) | copy-start | bytes 49156
  407.7 98.5 %all-gather.9.cloned.1.call-start = ((), (), s32[]{:S(2)}) async-start(), calls=%async_computation.9 | async-start | bytes 9437184 | tf_op jit(solution)/shard_map/all_gather | solution.py:85
  408.3 345.4 %reduce-scatter.7.cloned.1.call-start = ((), (), s32[]{:S(2)}) async-start(), calls=%async_computation.6 | async-start | bytes 9437184 | tf_op jit(solution)/shard_map/reduce_scatter | solution.py:79
  464.8 52.0 %copy-start.36 = (f32[32,32,2,256]{3,1,2,0:T(8,128)}, f32[32,32,2,256]{3,1,2,0:T(8,128)S(1)}, u32[]{:S(2)}) copy-start(f32[32,32,2,256]{3,1,2,0:T(8,128)S(1)} %fusion.241) | copy-start | bytes 6291460
  547.9 17.6 %copy-start.62 = (pred[32,64]{1,0:T(8,128)(4,1)S(1)}, pred[32,64]{1,0:T(8,128)(4,1)}, u32[]{:S(2)}) copy-start(pred[32,64]{1,0:T(8,128)(4,1)} %copy-done.61) | copy-start | bytes 6148
  553.0 17.7 %copy-start.53 = (pred[32,32,64]{2,1,0:T(8,128)(4,1)S(1)}, pred[32,32,64]{2,1,0:T(8,128)(4,1)}, u32[]{:S(2)}) copy-start(pred[32,32,64]{2,1,0:T(8,128)(4,1)} %copy-done.52) | copy-start | bytes 196612
  588.8 21.4 %copy-start.70 = (f32[1,2048]{1,0:T(1,128)S(1)}, f32[1,2048]{1,0:T(1,128)}, u32[]{:S(2)}) copy-start(f32[1,2048]{1,0:T(1,128)} %get-tuple-element.71) | copy-start | bytes 24580
  610.2 26.3 %copy-start.54 = (bf16[128,8,2,256]{3,1,2,0:T(8,128)(2,1)S(1)}, bf16[128,8,2,256]{3,1,2,0:T(8,128)(2,1)}, u32[]{:S(2)}) copy-start(bf16[128,8,2,256]{3,1,2,0:T(8,128)(2,1)} %copy.104) | copy-start | bytes 3145732
  648.1 167.9 %reduce-scatter.11.cloned.1.call-start = ((), (), s32[]{:S(2)}) async-start(), calls=%async_computation.10 | async-start | bytes 9437184 | tf_op jit(solution)/shard_map/reduce_scatter | solution.py:79
  661.1 18.7 %copy-start.21 = (bf16[1,32,64,2,256]{4,3,2,1,0:T(2,128)(2,1)S(1)}, bf16[1,32,64,2,256]{4,3,2,1,0:T(2,128)(2,1)}, u32[]{:S(2)}) copy-start(bf16[1,32,64,2,256]{4,3,2,1,0:T(2,128)(2,1)} %get-tuple-element.22) | copy-start | bytes 6291460
  661.1 18.7 %copy-start.56 = (s32[32,32]{1,0:T(8,128)S(1)}, s32[32,32]{1,0:T(8,128)}, u32[]{:S(2)}) copy-start(s32[32,32]{1,0:T(8,128)} %copy-done.55) | copy-start | bytes 12292
  661.2 18.7 %copy-start.60 = (pred[32,64]{1,0:T(8,128)(4,1)S(1)}, pred[32,64]{1,0:T(8,128)(4,1)}, u32[]{:S(2)}) copy-start(pred[32,64]{1,0:T(8,128)(4,1)} %copy-done.59) | copy-start | bytes 6148
  687.3 28.9 %copy-start.18 = (bf16[32,64,2,256]{3,1,2,0:T(8,128)(2,1)}, bf16[32,64,2,256]{3,1,2,0:T(8,128)(2,1)S(1)}, u32[]{:S(2)}) copy-start(bf16[32,64,2,256]{3,1,2,0:T(8,128)(2,1)S(1)} %fusion.140) | copy-start | bytes 6291460
  753.6 62.5 %copy-start.9 = (bf16[128,4096]{1,0:T(8,128)(2,1)S(1)}, bf16[128,4096]{1,0:T(8,128)(2,1)}, u32[]{:S(2)}) copy-start(bf16[128,4096]{1,0:T(8,128)(2,1)} %copy-done.8) | copy-start | bytes 3145732
  753.6 62.5 %copy-start.65 = (f32[1,4096]{1,0:T(1,128)S(1)}, f32[1,4096]{1,0:T(1,128)}, u32[]{:S(2)}) copy-start(f32[1,4096]{1,0:T(1,128)} %get-tuple-element.65) | copy-start | bytes 49156
  753.6 67.2 %copy-start.2 = (bf16[32,64,2,256]{3,1,2,0:T(8,128)(2,1)S(1)}, bf16[32,64,2,256]{3,1,2,0:T(8,128)(2,1)}, u32[]{:S(2)}) copy-start(bf16[32,64,2,256]{3,1,2,0:T(8,128)(2,1)} %copy-done.1) | copy-start | bytes 6291460
  753.6 124.3 %all-gather.7.cloned.1.call-start = ((), (), s32[]{:S(2)}) async-start(), calls=%async_computation.7 | async-start | bytes 9437184 | tf_op jit(solution)/shard_map/all_gather | solution.py:85
  820.0 98.7 %all-gather.11.cloned.1.call-start = ((), (), s32[]{:S(2)}) async-start(), calls=%async_computation.11 | async-start | bytes 9437184 | tf_op jit(solution)/shard_map/all_gather | solution.py:85
  (67 other events, 599.1 us)
Sparse Core Ops, SparseCore 0:
  211.2 65.0 reduce-scatter.8
  336.1 65.0 reduce-scatter.4
  407.8 48.3 all-gather.4
  457.8 48.3 all-gather.8
  648.2 62.2 reduce-scatter.6
  753.7 62.2 reduce-scatter.10
  820.2 48.3 all-gather.6
  870.3 48.3 all-gather.10

commit v2 on v0

v2 whole, which is shorter than its diff:
```python
import functools

import jax
import jax.numpy as jnp
from jax import lax
from jax.experimental import pallas as pl
from jax.experimental.pallas import tpu as pltpu
from jax.sharding import PartitionSpec as P

MESH = pl.DeviceIdType.MESH
ROT_DIM = 64
LN_EPS = 1e-5
GELU_C = 0.7978845608028654
WIDTH, HEAD, STEPS, SLOTS, HEADS = 4096, 256, 32, 64, 2
GROUP = 16
N_GROUPS, N_LAYERS = 4, 2
N_TASKS = N_GROUPS * N_LAYERS
ROWS = STEPS * GROUP
FF, ATT = 2048, 512
TILE = 256
T_QKV, T_IN, T_OUT = 3 * ATT // TILE, FF // TILE, WIDTH // TILE
T_ALL = T_QKV + T_IN + T_OUT
NBUF = 4
RS0, RS1, RS2, AGA, AGB, AGC = range(6)


def norm_rows(x, gain, bias):
    mean = jnp.mean(x, axis=-1, keepdims=True)
    centered = x - mean
    var = jnp.mean(centered * centered, axis=-1, keepdims=True)
    return (centered * lax.rsqrt(var + LN_EPS) * gain + bias).astype(jnp.bfloat16)


def kernel(cur_ref, x_hbm, kc_hbm, vc_hbm, gain_ref, bias_ref, bout_ref, bin_ref, cos_ref, sin_ref,
           wq, wk, wv, wo, win, wout, out_hbm, ko_hbm, vo_hbm,
           hbuf, gbuf, pbuf, r0, r1, r2, xres, qkv, ctx, act, wbuf, kbuf, vbuf,
           wsem, hsem, csem, cosem, xsem, gsem, ssem, rsem, ready, r0free):
    me = lax.axis_index("tp")
    core = me % 2
    xc = (me // 2) % 2
    yc = me // 4
    sib = me + 1 - 2 * core
    xn = me + 2 - 4 * xc
    yn = me + 4 - 8 * yc
    a1 = (1 - core) * xc + core * yc
    a2 = (1 - core) * yc + core * xc
    p1 = (1 - core) * xn + core * yn
    p2 = (1 - core) * yn + core * xn
    half = 16 * core
    quarter = half + 8 * a1
    own = quarter + 4 * a2
    partners = (sib, p1, p2)

    barrier = pltpu.get_barrier_semaphore()
    for dev in partners:
        pl.semaphore_signal(barrier, inc=1, device_id={"tp": dev}, device_id_type=MESH)
    pl.semaphore_wait(barrier, 3)

    def remote(src, dst, idx, dev):
        return pltpu.make_async_remote_copy(src_ref=src, dst_ref=dst, send_sem=ssem.at[idx], recv_sem=rsem.at[idx],
                                            device_id={"tp": dev}, device_id_type=MESH)

    def issue(u):
        @pl.when(u < N_TASKS * T_ALL)
        def _():
            task, j = u // T_ALL, u % T_ALL
            layer = task // N_GROUPS
            b = u % NBUF
            for k, ref in enumerate((wq, wk, wv)):
                @pl.when((j >= 2 * k) & (j < 2 * k + 2))
                def _():
                    col = pl.multiple_of((j - 2 * k) * TILE, TILE)
                    pltpu.make_async_copy(ref.at[layer, :, pl.ds(col, TILE)], wbuf.at[b], wsem.at[b]).start()

            @pl.when((j >= T_QKV) & (j < T_QKV + T_IN))
            def _():
                col = pl.multiple_of((j - T_QKV) * TILE, TILE)
                pltpu.make_async_copy(win.at[layer, :, pl.ds(col, TILE)], wbuf.at[b], wsem.at[b]).start()

            @pl.when(j >= T_QKV + T_IN)
            def _():
                col = pl.multiple_of((j - T_QKV - T_IN) * TILE, TILE)
                pltpu.make_async_copy(wo.at[layer, :, pl.ds(col, TILE)], wbuf.at[b, pl.ds(0, ATT), :], wsem.at[b]).start()
                pltpu.make_async_copy(wout.at[layer, :, pl.ds(col, TILE)], wbuf.at[b, pl.ds(ATT, FF), :], wsem.at[b]).start()

    def load_h(task):
        c = task % N_GROUPS
        b = task % 2
        cols = pl.ds(pl.multiple_of(c * GROUP, GROUP), GROUP)

        @pl.when(task < N_GROUPS)
        def _():
            pltpu.make_async_copy(x_hbm.at[:, cols, :], hbuf.at[b], hsem.at[b]).start()

        @pl.when((task >= N_GROUPS) & (task < N_TASKS))
        def _():
            pltpu.make_async_copy(out_hbm.at[:, cols, :], hbuf.at[b], hsem.at[b]).start()

    def add_rows(p, base, r_ref, rbase, n):
        def body(t, _):
            pbuf[p, base + t] = (pbuf[p, base + t].astype(jnp.float32) + r_ref[rbase + t].astype(jnp.float32)).astype(jnp.bfloat16)
            return 0
        lax.fori_loop(0, n, body, 0)

    for u in range(NBUF):
        issue(u)
    load_h(0)

    row_i = lax.broadcasted_iota(jnp.int32, (2 * SLOTS, 2 * STEPS), 0)
    col_i = lax.broadcasted_iota(jnp.int32, (2 * SLOTS, 2 * STEPS), 1)
    put_same = (row_i % 2) == (col_i // STEPS)
    put_off = row_i // 2 - col_i % STEPS
    wr_slot = lax.broadcasted_iota(jnp.int32, (2 * SLOTS, HEAD), 0) // 2
    s_row = lax.broadcasted_iota(jnp.int32, (2 * STEPS, 2 * SLOTS), 0)
    s_col = lax.broadcasted_iota(jnp.int32, (2 * STEPS, 2 * SLOTS), 1)
    see_same = (s_row // STEPS) == (s_col % 2)
    see_off = s_col // 2 - s_row % STEPS
    even_lane = lax.broadcasted_iota(jnp.int32, (STEPS, 128), 1) % 2 == 0

    def slot(s, _):
        pn, po = s % 2, (s + 1) % 2
        gb, gn = s % 2, (s + 1) % 2
        hb = s % 2
        layer, c = s // N_GROUPS, s % N_GROUPS
        l1, c1 = (s + N_GROUPS - 1) // N_GROUPS - 1, (s + N_GROUPS - 1) % N_GROUPS
        c2 = (s + N_GROUPS - 2) % N_GROUPS
        do_c = s < N_TASKS
        do_rs = (s >= 1) & (s <= N_TASKS)
        do_ag = s >= 2
        cseq = pl.multiple_of(c * GROUP, GROUP)

        def mm1_tile(j):
            u = s * T_ALL + j
            b = u % NBUF
            pltpu.make_async_copy(win.at[0, :, pl.ds(0, TILE)], wbuf.at[b], wsem.at[b]).wait()
            acc = jnp.dot(hbuf[hb].reshape(ROWS, WIDTH), wbuf[b], preferred_element_type=jnp.float32)
            return acc, u

        @pl.when(do_rs)
        def _():
            remote(pbuf.at[po, pl.ds(16 - half, 16)], r0, RS0, sib).wait()
            add_rows(po, half + 8 * (1 - a1), r0, 8 * (1 - a1), 8)

        @pl.when(s >= 1)
        def _():
            pl.semaphore_wait(ready.at[1], 1)
            pl.semaphore_wait(ready.at[2], 1)

        @pl.when(do_ag)
        def _():
            remote(gbuf.at[gb, pl.ds(own, 4)], gbuf.at[gb, pl.ds(own, 4)], AGA, p2).start()

        @pl.when(do_rs)
        def _():
            remote(pbuf.at[po, pl.ds(half + 8 * (1 - a1), 8)], r1, RS1, p1).start()
            add_rows(po, quarter, r0, 8 * a1, 8)

        @pl.when((s >= 1) & (s < N_TASKS))
        def _():
            pl.semaphore_signal(r0free, inc=1, device_id={"tp": sib}, device_id_type=MESH)

        @pl.when(do_c)
        def _():
            @pl.when(s >= 1)
            def _():
                pltpu.make_async_copy(kbuf, ko_hbm.at[0, pl.ds(0, GROUP)], cosem.at[0]).wait()
                pltpu.make_async_copy(vbuf, vo_hbm.at[0, pl.ds(0, GROUP)], cosem.at[1]).wait()
            pltpu.make_async_copy(kc_hbm.at[layer, pl.ds(cseq, GROUP)], kbuf, csem.at[0]).start()
            pltpu.make_async_copy(vc_hbm.at[layer, pl.ds(cseq, GROUP)], vbuf, csem.at[1]).start()
            pltpu.make_async_copy(x_hbm.at[:, pl.ds(0, GROUP), :], hbuf.at[hb], hsem.at[hb]).wait()

            @pl.when(layer == 0)
            def _():
                def ln(t, _):
                    hbuf[hb, t] = norm_rows(hbuf[hb, t].astype(jnp.float32), gain_ref[0], bias_ref[0])
                    return 0
                lax.fori_loop(0, STEPS, ln, 0)

            def qkv_tile(j, _):
                acc, u = mm1_tile(j)
                qkv[2 * j] = acc[:, :128]
                qkv[2 * j + 1] = acc[:, 128:]
                issue(u + NBUF)
                return 0
            lax.fori_loop(0, T_QKV, qkv_tile, 0)

        @pl.when(do_ag)
        def _():
            remote(gbuf.at[gb, pl.ds(own, 4)], gbuf.at[gb, pl.ds(own, 4)], AGA, p2).wait()
            remote(gbuf.at[gb, pl.ds(quarter, 8)], gbuf.at[gb, pl.ds(quarter, 8)], AGB, p1).start()

        @pl.when(s >= 3)
        def _():
            pltpu.make_async_copy(gbuf.at[gn], out_hbm.at[:, pl.ds(0, GROUP), :], gsem).wait()

        load_h(s + 1)

        @pl.when(do_rs & (l1 == 0))
        def _():
            pltpu.make_async_copy(x_hbm.at[pl.ds(own, 4), pl.ds(pl.multiple_of(c1 * GROUP, GROUP), GROUP), :], xres.at[c1], xsem).start()

        def in_tile(j, _):
            acc, u = mm1_tile(T_QKV + j)
            y = acc + bin_ref[layer, j]
            g = 0.5 * y * (1.0 + jnp.tanh(GELU_C * (y + 0.044715 * y * y * y)))
            act[:, pl.ds(pl.multiple_of(ATT + j * TILE, TILE), TILE)] = g.astype(jnp.bfloat16)
            issue(u + NBUF)
            return 0

        @pl.when(do_c)
        def _():
            lax.fori_loop(0, T_IN // 2, in_tile, 0)

        @pl.when(do_rs)
        def _():
            remote(pbuf.at[po, pl.ds(half + 8 * (1 - a1), 8)], r1, RS1, p1).wait()
            add_rows(po, quarter + 4 * (1 - a2), r1, 4 * (1 - a2), 4)
            remote(pbuf.at[po, pl.ds(quarter + 4 * (1 - a2), 4)], r2, RS2, p2).start()
            add_rows(po, own, r1, 4 * a2, 4)

        def attend(i, _):
            b = c * GROUP + i
            cur = cur_ref[b]
            cos_t, sin_t = cos_ref[b], sin_ref[b]

            def part(k, rotary):
                lo = qkv[2 * k, pl.ds(i, STEPS, stride=GROUP), :]
                hi = qkv[2 * k + 1, pl.ds(i, STEPS, stride=GROUP), :]
                if rotary:
                    other = jnp.where(even_lane, pltpu.roll(lo, 127, 1), pltpu.roll(lo, 1, 1))
                    lo = lo * cos_t + other * sin_t
                return jnp.concatenate([lo, hi], axis=1)

            q = jnp.concatenate([part(0, True), part(1, True)], axis=0).astype(jnp.bfloat16)
            k_new = jnp.concatenate([part(2, True), part(3, True)], axis=0).astype(jnp.bfloat16)
            v_new = jnp.concatenate([part(4, False), part(5, False)], axis=0).astype(jnp.bfloat16)
            put = jnp.where(put_same & (put_off == cur), 1.0, 0.0).astype(jnp.bfloat16)
            written = (wr_slot >= cur) & (wr_slot < cur + STEPS)
            k_all = jnp.where(written, jnp.dot(put, k_new, preferred_element_type=jnp.float32), kbuf[i].astype(jnp.float32)).astype(jnp.bfloat16)
            v_all = jnp.where(written, jnp.dot(put, v_new, preferred_element_type=jnp.float32), vbuf[i].astype(jnp.float32)).astype(jnp.bfloat16)
            kbuf[i] = k_all
            vbuf[i] = v_all
            sc = lax.dot_general(q, k_all, (((1,), (1,)), ((), ())), preferred_element_type=jnp.float32) * (HEAD ** -0.5)
            sc = jnp.where(see_same & (see_off <= cur), sc, -jnp.inf)
            ex = jnp.exp(sc - jnp.max(sc, axis=-1, keepdims=True))
            pr = (ex / jnp.sum(ex, axis=-1, keepdims=True)).astype(jnp.bfloat16)
            cx = jnp.dot(pr, v_all, preferred_element_type=jnp.float32)
            for h in range(HEADS):
                for w in range(2):
                    ctx[2 * h + w, pl.ds(i, STEPS, stride=GROUP), :] = cx[h * STEPS:(h + 1) * STEPS, w * 128:(w + 1) * 128]
            return 0

        def out_tile(j, _):
            u = s * T_ALL + T_QKV + T_IN + j
            b = u % NBUF
            pltpu.make_async_copy(win.at[0, pl.ds(0, ATT + FF), pl.ds(0, TILE)], wbuf.at[b, pl.ds(0, ATT + FF), :], wsem.at[b]).wait()
            acc = jnp.dot(act[...], wbuf[b, :ATT + FF, :], preferred_element_type=jnp.float32)
            pbuf[pn, :, :, pl.ds(pl.multiple_of(j * TILE, TILE), TILE)] = acc.astype(jnp.bfloat16).reshape(STEPS, GROUP, TILE)

            @pl.when(j >= 1)
            def _():
                send_half(j - 1)
            issue(u + NBUF)
            return 0

        def send_half(j):
            cols = pl.ds(pl.multiple_of(j * TILE, TILE), TILE)
            remote(pbuf.at[pn, pl.ds(16 - half, 16), :, cols], r0.at[:, :, cols], RS0, sib).start()

        @pl.when(do_c)
        def _():
            lax.fori_loop(T_IN // 2, T_IN, in_tile, 0)
            pltpu.make_async_copy(kc_hbm.at[0, pl.ds(0, GROUP)], kbuf, csem.at[0]).wait()
            pltpu.make_async_copy(vc_hbm.at[0, pl.ds(0, GROUP)], vbuf, csem.at[1]).wait()
            lax.fori_loop(0, GROUP, attend, 0)
            pltpu.make_async_copy(kbuf, ko_hbm.at[layer, pl.ds(cseq, GROUP)], cosem.at[0]).start()
            pltpu.make_async_copy(vbuf, vo_hbm.at[layer, pl.ds(cseq, GROUP)], cosem.at[1]).start()
            for k in range(4):
                act[:, k * 128:(k + 1) * 128] = ctx[k].astype(jnp.bfloat16)

            @pl.when(s >= 1)
            def _():
                pl.semaphore_wait(r0free, 1)
            lax.fori_loop(0, T_OUT // 2, out_tile, 0)

        @pl.when(do_rs)
        def _():
            remote(pbuf.at[po, pl.ds(quarter + 4 * (1 - a2), 4)], r2, RS2, p2).wait()

            @pl.when(l1 == 0)
            def _():
                pltpu.make_async_copy(x_hbm.at[pl.ds(0, 4), pl.ds(0, GROUP), :], xres.at[c1], xsem).wait()

            def finish(t, _):
                tot = pbuf[po, own + t].astype(jnp.float32) + r2[t].astype(jnp.float32)
                new = (xres[c1, t].astype(jnp.float32) + tot + bout_ref[l1]).astype(jnp.bfloat16)

                @pl.when(l1 == 0)
                def _():
                    xres[c1, t] = new
                    gbuf[gn, own + t] = norm_rows(new.astype(jnp.float32), gain_ref[1], bias_ref[1])

                @pl.when(l1 == 1)
                def _():
                    gbuf[gn, own + t] = new
                return 0
            lax.fori_loop(0, 4, finish, 0)

        @pl.when(do_ag)
        def _():
            remote(gbuf.at[gb, pl.ds(quarter, 8)], gbuf.at[gb, pl.ds(quarter, 8)], AGB, p1).wait()

        @pl.when(s <= N_TASKS)
        def _():
            for k in (1, 2):
                pl.semaphore_signal(ready.at[k], inc=1, device_id={"tp": partners[k]}, device_id_type=MESH)

        @pl.when(s >= 1)
        def _():
            pl.semaphore_wait(ready.at[0], 1)

        @pl.when(do_ag)
        def _():
            remote(gbuf.at[gb, pl.ds(half, 16)], gbuf.at[gb, pl.ds(half, 16)], AGC, sib).start()

        @pl.when(do_c)
        def _():
            lax.fori_loop(T_OUT // 2, T_OUT, out_tile, 0)
            send_half(T_OUT - 1)

        @pl.when(do_ag)
        def _():
            remote(gbuf.at[gb, pl.ds(half, 16)], gbuf.at[gb, pl.ds(half, 16)], AGC, sib).wait()
            pltpu.make_async_copy(gbuf.at[gb], out_hbm.at[:, pl.ds(pl.multiple_of(c2 * GROUP, GROUP), GROUP), :], gsem).start()

        @pl.when(s <= N_TASKS)
        def _():
            pl.semaphore_signal(ready.at[0], inc=1, device_id={"tp": sib}, device_id_type=MESH)
        return 0

    lax.fori_loop(0, N_TASKS + 2, slot, 0)
    pltpu.make_async_copy(gbuf.at[0], out_hbm.at[:, pl.ds(0, GROUP), :], gsem).wait()
    pltpu.make_async_copy(kbuf, ko_hbm.at[0, pl.ds(0, GROUP)], cosem.at[0]).wait()
    pltpu.make_async_copy(vbuf, vo_hbm.at[0, pl.ds(0, GROUP)], cosem.at[1]).wait()


def decode_shard(x_steps, cur_len, k_cache, v_cache, ln_gain, ln_bias, w_q, w_k, w_v, w_o, w_in, b_in, w_out, b_out):
    n_layers, batch, slots, heads, dim = k_cache.shape
    f32 = jnp.float32
    lane = jnp.arange(128)
    inv_freq = jnp.where(lane < ROT_DIM, 1.0 / (10000.0 ** ((lane // 2 * 2).astype(f32) / ROT_DIM)), 0.0)
    pos = (cur_len[:, None] + jnp.arange(STEPS)[None, :]).astype(f32)
    angles = pos[:, :, None] * inv_freq
    cos_tab = jnp.cos(angles)
    sin_tab = jnp.sin(angles) * jnp.where(lane % 2 == 0, -1.0, 1.0)
    flat = (n_layers, batch, slots * heads, dim)
    bf = jnp.bfloat16
    any_spec, vmem = pl.BlockSpec(memory_space=pl.ANY), pl.BlockSpec(memory_space=pltpu.VMEM)
    out, k_out, v_out = pl.pallas_call(
        kernel,
        out_shape=(jax.ShapeDtypeStruct(x_steps.shape, bf), jax.ShapeDtypeStruct(flat, bf), jax.ShapeDtypeStruct(flat, bf)),
        in_specs=[pl.BlockSpec(memory_space=pltpu.SMEM), any_spec, any_spec, any_spec] + [vmem] * 6 + [any_spec] * 6,
        out_specs=(any_spec, any_spec, any_spec),
        scratch_shapes=[
            pltpu.VMEM((2, STEPS, GROUP, WIDTH), bf),
            pltpu.VMEM((2, STEPS, GROUP, WIDTH), bf),
            pltpu.VMEM((2, STEPS, GROUP, WIDTH), bf),
            pltpu.VMEM((16, GROUP, WIDTH), bf),
            pltpu.VMEM((8, GROUP, WIDTH), bf),
            pltpu.VMEM((4, GROUP, WIDTH), bf),
            pltpu.VMEM((N_GROUPS, 4, GROUP, WIDTH), bf),
            pltpu.VMEM((12, ROWS, 128), f32),
            pltpu.VMEM((4, ROWS, 128), f32),
            pltpu.VMEM((ROWS, ATT + FF), bf),
            pltpu.VMEM((NBUF, WIDTH, TILE), bf),
            pltpu.VMEM((GROUP, 2 * SLOTS, HEAD), bf),
            pltpu.VMEM((GROUP, 2 * SLOTS, HEAD), bf),
            pltpu.SemaphoreType.DMA((NBUF,)),
            pltpu.SemaphoreType.DMA((2,)),
            pltpu.SemaphoreType.DMA((2,)),
            pltpu.SemaphoreType.DMA((2,)),
            pltpu.SemaphoreType.DMA,
            pltpu.SemaphoreType.DMA,
            pltpu.SemaphoreType.DMA((6,)),
            pltpu.SemaphoreType.DMA((6,)),
            pltpu.SemaphoreType.REGULAR((3,)),
            pltpu.SemaphoreType.REGULAR,
        ],
        compiler_params=pltpu.CompilerParams(collective_id=0, has_side_effects=True, vmem_limit_bytes=62 * 1024 * 1024),
    )(cur_len, x_steps, k_cache.reshape(flat), v_cache.reshape(flat),
      ln_gain.astype(f32)[:, None], ln_bias.astype(f32)[:, None], b_out.astype(f32)[:, None],
      b_in.astype(f32).reshape(n_layers, T_IN, 1, TILE), cos_tab, sin_tab, w_q, w_k, w_v, w_o, w_in, w_out)
    return out, k_out.reshape(k_cache.shape), v_out.reshape(v_cache.shape)


def solution(mesh):
    cache_spec = P(None, "dp", None, "tp", None)
    in_specs = (P(None, "dp", None), P("dp"), cache_spec, cache_spec, P(None, None), P(None, None),
                P(None, None, "tp"), P(None, None, "tp"), P(None, None, "tp"), P(None, "tp", None),
                P(None, None, "tp"), P(None, "tp"), P(None, "tp", None), P(None, None))
    out_specs = (P(None, "dp", None), cache_spec, cache_spec)
    return jax.shard_map(decode_shard, mesh=mesh, in_specs=in_specs, out_specs=out_specs, check_vma=False)
```

time: 6600 us -> 591 us (0.09)
  local copies, waits for them, and re-layouts: 2760 us -> 71.6 us
  matrix products: 2020 us -> 0 us
  waiting for transfers between devices: 1450 us -> 0 us
  Pallas kernels: 0 us -> 510 us
  other arithmetic: 297 us -> 6.26 us
    dot_general x448 -> x0, matrix products: 2020 us -> none  [the longest x64 932 us: layer_update(): jnp.dot(gelu_act, out_weight, preferred_element_type=jnp.float32)]
    psum x33 -> x0, waiting for transfers between devices: 1450 us -> none  [decode_shard(): layer_sum = lax.psum(layer_part.astype(jnp.bfloat16), 'tp')]
    squeeze x128 -> x0, local copies, waits for them, and re-layouts: 1330 us -> none  [the longest x64 669 us: layer_update(): v_cache[layer_idx]]
    scatter x128 -> x0, local copies, waits for them, and re-layouts: 1180 us -> none  [the longest x64 599 us: layer_update(): v_cache = v_cache.at[layer_idx, batch_rows, new_pos].set(value_new)]
    pallas_call x0 -> x1, Pallas kernels: none -> 510 us  [decode_shard(): pl.pallas_call(kernel, out_shape=(jax.ShapeDtypeStruct(x_steps.shape, bf)...]
    reduce_sum x70 -> x0, other arithmetic: 83.6 us -> none  [the longest x34 61.2 us: layer_norm(): row_mean = jnp.mean(hid_f32, axis=-1, keepdims=True)]
    slice x437 -> x0, local copies, waits for them, and re-layouts: 81.5 us -> none  [the longest x128 48 us: apply_rotary(): vectors[..., ROT_DIM:]]
    concatenate x129 -> x0, other arithmetic: 67.9 us -> none  [the longest x128 66.9 us: apply_rotary(): jnp.concatenate([rotated.reshape(lead_shape + (ROT_DIM,)), vectors[..., R...]
  transfers between devices with their start and end apart: 33 -> 0, of which waited for: 32 -> 0; matrix products, arithmetic and copies ran while one was open for 17% -> 0% of each run, Pallas kernels for 0% -> 0%
where the time goes in v2:
time: 591 us; the launch traced here: 589 us
  Pallas kernels  510 us (86%)
  local copies, waits for them, and re-layouts  71.6 us (12%)
  other arithmetic  6.26 us (1%)
    pallas_call x1, Pallas kernels, decode_shard(): pl.pallas_call(kernel, out_shape=(jax.ShapeDtypeStruct(x_steps.shape, bf)...  510 us
    reshape x2, local copies, waits for them, and re-layouts, decode_shard(): return (out, k_out.reshape(k_cache.shape), v_out.reshape(v_cache.shape))  26.1 us
    unnamed x1, local copies, waits for them, and re-layouts  14.1 us
    reshape x1, local copies, waits for them, and re-layouts, decode_shard(): k_cache.reshape(flat)  13.1 us
    reshape x1, local copies, waits for them, and re-layouts, decode_shard(): v_cache.reshape(flat)  13.1 us

profile of v2, /device:TPU:0, one launch (start us, length us, event | category | flops | bytes accessed | tf_op | source)
XLA Modules:
  0.0 589.0 jit_solution(6129226810055940688)
XLA Ops:
  0.6 1.3 reshape.87.bin_ref
  2.0 1.3 reshape.83.gain_ref
  3.3 1.3 reshape.84.bias_ref
  4.6 1.4 reshape.85.bout_ref
  6.0 0.7 add_convert_fusion
  6.7 5.5 fusion
  12.2 13.1 %reshape.77.kc_hbm = bf16[2,64,128,256]{3,2,1,0:T(8,128)(2,1)} reshape(bf16[2,64,64,2,256]{4,3,2,1,0:T(2,128)(2,1)} %param.16) | data formatting | bytes 16777216 | tf_op jit(solution)/shard_map/reshape | solution.py:390
  25.3 13.1 %reshape.78.vc_hbm = bf16[2,64,128,256]{3,2,1,0:T(8,128)(2,1)} reshape(bf16[2,64,64,2,256]{4,3,2,1,0:T(2,128)(2,1)} %param.17) | data formatting | bytes 16777216 | tf_op jit(solution)/shard_map/reshape | solution.py:390
  38.4 510.5 %shard_map.157 = (bf16[32,64,4096]{2,1,0:T(8,128)(2,1)}, bf16[2,64,128,256]{3,2,1,0:T(8,128)(2,1)}, bf16[2,64,128,256]{3,2,1,0:T(8,128)(2,1)}) custom-call(s32[64]{0:T(128)} %cur_ref.1, bf16[32,64,4096]{2,1,0:T(8,128)(2,1)} %x_hbm.1, bf16[2,64,128,256]{3,2,1,0:T(8,128)(2,1)} %reshape.77.kc_hbm, bf16[2,64,128,256]{3,2,1,0:T(8,128)(2,1)} %reshape.78.vc_hbm, ...), custom_call_target="tpu_custom_call" | custom-call | tf_op jit(solution)/shard_map/pallas_call | solution.py:359
  548.8 13.1 %reshape.81 = bf16[2,64,64,2,256]{4,3,2,1,0:T(2,128)(2,1)} reshape(bf16[2,64,128,256]{3,2,1,0:T(8,128)(2,1)} %get-tuple-element.7) | data formatting | bytes 16777216 | tf_op jit(solution)/shard_map/reshape | solution.py:393
  561.9 13.1 %reshape.82 = bf16[2,64,64,2,256]{4,3,2,1,0:T(2,128)(2,1)} reshape(bf16[2,64,128,256]{3,2,1,0:T(8,128)(2,1)} %get-tuple-element.8) | data formatting | bytes 16777216 | tf_op jit(solution)/shard_map/reshape | solution.py:393
  574.9 14.1 %copy.18 = bf16[32,64,4096]{2,1,0:T(8,128)(2,1)} copy(bf16[32,64,4096]{2,1,0:T(8,128)(2,1)} %get-tuple-element.16) | data formatting | bytes 33554432
  (1 shorter events, 0.0 us)

commit v3 on v2

--- a/solution.py
+++ b/solution.py
@@ -2,6 +2,7 @@
 
 import jax
 import jax.numpy as jnp
+import numpy as np
 from jax import lax
 from jax.experimental import pallas as pl
 from jax.experimental.pallas import tpu as pltpu
@@ -17,10 +18,13 @@
 N_TASKS = N_GROUPS * N_LAYERS
 ROWS = STEPS * GROUP
 FF, ATT = 2048, 512
-TILE = 256
+TILE = 512
 T_QKV, T_IN, T_OUT = 3 * ATT // TILE, FF // TILE, WIDTH // TILE
 T_ALL = T_QKV + T_IN + T_OUT
-NBUF = 4
+NBUF = 3
+LN_STEP = 4
+AT_STEP = 4
+TOP_TILES, OUT_SPLIT = 1, 6
 RS0, RS1, RS2, AGA, AGB, AGC = range(6)
 
 
@@ -31,10 +35,10 @@
     return (centered * lax.rsqrt(var + LN_EPS) * gain + bias).astype(jnp.bfloat16)
 
 
-def kernel(cur_ref, x_hbm, kc_hbm, vc_hbm, gain_ref, bias_ref, bout_ref, bin_ref, cos_ref, sin_ref,
+def kernel(cur_ref, x_hbm, kc_hbm, vc_hbm, gain_in, bias_in, bout_in, bin_in, cos_ref, sin_ref,
            wq, wk, wv, wo, win, wout, out_hbm, ko_hbm, vo_hbm,
-           hbuf, gbuf, pbuf, r0, r1, r2, xres, qkv, ctx, act, wbuf, kbuf, vbuf,
-           wsem, hsem, csem, cosem, xsem, gsem, ssem, rsem, ready, r0free):
+           hbuf, gbuf, pbuf, r0, r1, r2, xres, qkv, ctx, act, wbuf, kbuf, vbuf, gain_ref, bias_ref, bout_ref, bin_ref,
+           wsem, hsem, csem, cosem, xsem, gsem, ssem, rsem, ready, r0free, gfree):
     me = lax.axis_index("tp")
     core = me % 2
     xc = (me // 2) % 2
@@ -67,9 +71,11 @@
             layer = task // N_GROUPS
             b = u % NBUF
             for k, ref in enumerate((wq, wk, wv)):
-                @pl.when((j >= 2 * k) & (j < 2 * k + 2))
+                n = ATT // TILE
+
+                @pl.when((j >= n * k) & (j < n * k + n))
                 def _():
-                    col = pl.multiple_of((j - 2 * k) * TILE, TILE)
+                    col = pl.multiple_of((j - n * k) * TILE, TILE)
                     pltpu.make_async_copy(ref.at[layer, :, pl.ds(col, TILE)], wbuf.at[b], wsem.at[b]).start()
 
             @pl.when((j >= T_QKV) & (j < T_QKV + T_IN))
@@ -105,6 +111,11 @@
     for u in range(NBUF):
         issue(u)
     load_h(0)
+    for l in range(N_LAYERS):
+        for dst, src in ((gain_ref, gain_in), (bias_ref, bias_in), (bout_ref, bout_in)):
+            dst[l] = src[l:l + 1, :].astype(jnp.float32)
+        for j in range(T_IN):
+            bin_ref[l, j] = bin_in[l:l + 1, j * TILE:(j + 1) * TILE].astype(jnp.float32)
 
     row_i = lax.broadcasted_iota(jnp.int32, (2 * SLOTS, 2 * STEPS), 0)
     col_i = lax.broadcasted_iota(jnp.int32, (2 * SLOTS, 2 * STEPS), 1)
@@ -136,28 +147,12 @@
             acc = jnp.dot(hbuf[hb].reshape(ROWS, WIDTH), wbuf[b], preferred_element_type=jnp.float32)
             return acc, u
 
-        @pl.when(do_rs)
-        def _():
-            remote(pbuf.at[po, pl.ds(16 - half, 16)], r0, RS0, sib).wait()
-            add_rows(po, half + 8 * (1 - a1), r0, 8 * (1 - a1), 8)
-
-        @pl.when(s >= 1)
-        def _():
-            pl.semaphore_wait(ready.at[1], 1)
-            pl.semaphore_wait(ready.at[2], 1)
-
-        @pl.when(do_ag)
-        def _():
-            remote(gbuf.at[gb, pl.ds(own, 4)], gbuf.at[gb, pl.ds(own, 4)], AGA, p2).start()
-
-        @pl.when(do_rs)
-        def _():
-            remote(pbuf.at[po, pl.ds(half + 8 * (1 - a1), 8)], r1, RS1, p1).start()
-            add_rows(po, quarter, r0, 8 * a1, 8)
-
-        @pl.when((s >= 1) & (s < N_TASKS))
-        def _():
-            pl.semaphore_signal(r0free, inc=1, device_id={"tp": sib}, device_id_type=MESH)
+        def qkv_tile(j, _):
+            acc, u = mm1_tile(j)
+            for w in range(TILE // 128):
+                qkv[TILE // 128 * j + w] = acc[:, w * 128:(w + 1) * 128]
+            issue(u + NBUF)
+            return 0
 
         @pl.when(do_c)
         def _():
@@ -172,26 +167,51 @@
             @pl.when(layer == 0)
             def _():
                 def ln(t, _):
-                    hbuf[hb, t] = norm_rows(hbuf[hb, t].astype(jnp.float32), gain_ref[0], bias_ref[0])
+                    done = [norm_rows(hbuf[hb, LN_STEP * t + k].astype(jnp.float32), gain_ref[0], bias_ref[0]) for k in range(LN_STEP)]
+                    for k in range(LN_STEP):
+                        hbuf[hb, LN_STEP * t + k] = done[k]
                     return 0
-                lax.fori_loop(0, STEPS, ln, 0)
-
-            def qkv_tile(j, _):
-                acc, u = mm1_tile(j)
-                qkv[2 * j] = acc[:, :128]
-                qkv[2 * j + 1] = acc[:, 128:]
-                issue(u + NBUF)
-                return 0
-            lax.fori_loop(0, T_QKV, qkv_tile, 0)
+                lax.fori_loop(0, STEPS // LN_STEP, ln, 0)
+
+            lax.fori_loop(0, TOP_TILES, qkv_tile, 0)
+
+        @pl.when(do_rs)
+        def _():
+            remote(pbuf.at[po, pl.ds(16 - half, 16)], r0, RS0, sib).wait()
+            add_rows(po, half + 8 * (1 - a1), r0, 8 * (1 - a1), 8)
+
+        @pl.when(s >= 1)
+        def _():
+            pl.semaphore_wait(ready.at[1], 1)
+
+        @pl.when(do_rs)
+        def _():
+            remote(pbuf.at[po, pl.ds(half + 8 * (1 - a1), 8)], r1, RS1, p1).start()
 
         @pl.when(do_ag)
         def _():
             remote(gbuf.at[gb, pl.ds(own, 4)], gbuf.at[gb, pl.ds(own, 4)], AGA, p2).wait()
             remote(gbuf.at[gb, pl.ds(quarter, 8)], gbuf.at[gb, pl.ds(quarter, 8)], AGB, p1).start()
 
+        @pl.when(do_rs)
+        def _():
+            add_rows(po, quarter, r0, 8 * a1, 8)
+
+        @pl.when((s >= 1) & (s < N_TASKS))
+        def _():
+            pl.semaphore_signal(r0free, inc=1, device_id={"tp": sib}, device_id_type=MESH)
+
+        @pl.when(do_c)
+        def _():
+            lax.fori_loop(TOP_TILES, T_QKV, qkv_tile, 0)
+
         @pl.when(s >= 3)
         def _():
             pltpu.make_async_copy(gbuf.at[gn], out_hbm.at[:, pl.ds(0, GROUP), :], gsem).wait()
+
+        @pl.when(do_rs)
+        def _():
+            pl.semaphore_signal(gfree, inc=1, device_id={"tp": p2}, device_id_type=MESH)
 
         load_h(s + 1)
 
@@ -209,45 +229,64 @@
 
         @pl.when(do_c)
         def _():
-            lax.fori_loop(0, T_IN // 2, in_tile, 0)
+            lax.fori_loop(0, T_IN, in_tile, 0)
 
         @pl.when(do_rs)
         def _():
             remote(pbuf.at[po, pl.ds(half + 8 * (1 - a1), 8)], r1, RS1, p1).wait()
             add_rows(po, quarter + 4 * (1 - a2), r1, 4 * (1 - a2), 4)
+
+        @pl.when(s >= 1)
+        def _():
+            pl.semaphore_wait(ready.at[2], 1)
+
+        @pl.when(do_rs)
+        def _():
             remote(pbuf.at[po, pl.ds(quarter + 4 * (1 - a2), 4)], r2, RS2, p2).start()
             add_rows(po, own, r1, 4 * a2, 4)
 
-        def attend(i, _):
-            b = c * GROUP + i
-            cur = cur_ref[b]
-            cos_t, sin_t = cos_ref[b], sin_ref[b]
-
-            def part(k, rotary):
+        def attend(step, _):
+            seqs = [AT_STEP * step + k for k in range(AT_STEP)]
+            curs = [cur_ref[c * GROUP + i] for i in seqs]
+
+            def part(i, k):
                 lo = qkv[2 * k, pl.ds(i, STEPS, stride=GROUP), :]
                 hi = qkv[2 * k + 1, pl.ds(i, STEPS, stride=GROUP), :]
-                if rotary:
-                    other = jnp.where(even_lane, pltpu.roll(lo, 127, 1), pltpu.roll(lo, 1, 1))
-                    lo = lo * cos_t + other * sin_t
-                return jnp.concatenate([lo, hi], axis=1)
-
-            q = jnp.concatenate([part(0, True), part(1, True)], axis=0).astype(jnp.bfloat16)
-            k_new = jnp.concatenate([part(2, True), part(3, True)], axis=0).astype(jnp.bfloat16)
-            v_new = jnp.concatenate([part(4, False), part(5, False)], axis=0).astype(jnp.bfloat16)
-            put = jnp.where(put_same & (put_off == cur), 1.0, 0.0).astype(jnp.bfloat16)
-            written = (wr_slot >= cur) & (wr_slot < cur + STEPS)
-            k_all = jnp.where(written, jnp.dot(put, k_new, preferred_element_type=jnp.float32), kbuf[i].astype(jnp.float32)).astype(jnp.bfloat16)
-            v_all = jnp.where(written, jnp.dot(put, v_new, preferred_element_type=jnp.float32), vbuf[i].astype(jnp.float32)).astype(jnp.bfloat16)
-            kbuf[i] = k_all
-            vbuf[i] = v_all
-            sc = lax.dot_general(q, k_all, (((1,), (1,)), ((), ())), preferred_element_type=jnp.float32) * (HEAD ** -0.5)
-            sc = jnp.where(see_same & (see_off <= cur), sc, -jnp.inf)
-            ex = jnp.exp(sc - jnp.max(sc, axis=-1, keepdims=True))
-            pr = (ex / jnp.sum(ex, axis=-1, keepdims=True)).astype(jnp.bfloat16)
-            cx = jnp.dot(pr, v_all, preferred_element_type=jnp.float32)
-            for h in range(HEADS):
-                for w in range(2):
-                    ctx[2 * h + w, pl.ds(i, STEPS, stride=GROUP), :] = cx[h * STEPS:(h + 1) * STEPS, w * 128:(w + 1) * 128]
+                return lo, hi
+
+            def turn(lo, hi, cos_t, sin_t):
+                other = jnp.where(even_lane, pltpu.roll(lo, 127, 1), pltpu.roll(lo, 1, 1))
+                return jnp.concatenate([lo * cos_t + other * sin_t, hi], axis=1)
+
+            def both(a, b):
+                return jnp.concatenate([a, b], axis=0).astype(jnp.bfloat16)
+
+            qs, ks, vs = [], [], []
+            for i, cur in zip(seqs, curs):
+                cos_t, sin_t = cos_ref[pl.ds(cur, STEPS), :], sin_ref[pl.ds(cur, STEPS), :]
+                qs.append(both(*[turn(*part(i, k), cos_t, sin_t) for k in (0, 1)]))
+                ks.append(both(*[turn(*part(i, k), cos_t, sin_t) for k in (2, 3)]))
+                vs.append(both(*[jnp.concatenate(part(i, k), axis=1) for k in (4, 5)]))
+            puts = [jnp.where(put_same & (put_off == cur), 1.0, 0.0).astype(jnp.bfloat16) for cur in curs]
+            writ = [(wr_slot >= cur) & (wr_slot < cur + STEPS) for cur in curs]
+
+            def merge(buf, new):
+                olds = [buf[i].reshape(2 * SLOTS, HEAD).astype(jnp.float32) for i in seqs]
+                put = [jnp.dot(p, n, preferred_element_type=jnp.float32) for p, n in zip(puts, new)]
+                return [jnp.where(w, p, o).astype(jnp.bfloat16) for w, p, o in zip(writ, put, olds)]
+
+            k_all, v_all = merge(kbuf, ks), merge(vbuf, vs)
+            sc = [lax.dot_general(q, k, (((1,), (1,)), ((), ())), preferred_element_type=jnp.float32) * (HEAD ** -0.5) for q, k in zip(qs, k_all)]
+            sc = [jnp.where(see_same & (see_off <= cur), x, -jnp.inf) for x, cur in zip(sc, curs)]
+            ex = [jnp.exp(x - jnp.max(x, axis=-1, keepdims=True)) for x in sc]
+            pr = [(e / jnp.sum(e, axis=-1, keepdims=True)).astype(jnp.bfloat16) for e in ex]
+            cx = [jnp.dot(p, v, preferred_element_type=jnp.float32) for p, v in zip(pr, v_all)]
+            for n, i in enumerate(seqs):
+                kbuf[i] = k_all[n].reshape(SLOTS, HEADS, HEAD)
+                vbuf[i] = v_all[n].reshape(SLOTS, HEADS, HEAD)
+                for h in range(HEADS):
+                    for w in range(2):
+                        ctx[2 * h + w, pl.ds(i, STEPS, stride=GROUP), :] = cx[n][h * STEPS:(h + 1) * STEPS, w * 128:(w + 1) * 128]
             return 0
 
         def out_tile(j, _):
@@ -269,10 +308,9 @@
 
         @pl.when(do_c)
         def _():
-            lax.fori_loop(T_IN // 2, T_IN, in_tile, 0)
             pltpu.make_async_copy(kc_hbm.at[0, pl.ds(0, GROUP)], kbuf, csem.at[0]).wait()
             pltpu.make_async_copy(vc_hbm.at[0, pl.ds(0, GROUP)], vbuf, csem.at[1]).wait()
-            lax.fori_loop(0, GROUP, attend, 0)
+            lax.fori_loop(0, GROUP // AT_STEP, attend, 0)
             pltpu.make_async_copy(kbuf, ko_hbm.at[layer, pl.ds(cseq, GROUP)], cosem.at[0]).start()
             pltpu.make_async_copy(vbuf, vo_hbm.at[layer, pl.ds(cseq, GROUP)], cosem.at[1]).start()
             for k in range(4):
@@ -281,7 +319,7 @@
             @pl.when(s >= 1)
             def _():
                 pl.semaphore_wait(r0free, 1)
-            lax.fori_loop(0, T_OUT // 2, out_tile, 0)
+            lax.fori_loop(0, OUT_SPLIT, out_tile, 0)
 
         @pl.when(do_rs)
         def _():
@@ -304,7 +342,10 @@
                 def _():
                     gbuf[gn, own + t] = new
                 return 0
-            lax.fori_loop(0, 4, finish, 0)
+            for t in range(4):
+                finish(t, 0)
+            pl.semaphore_wait(gfree, 1)
+            remote(gbuf.at[gn, pl.ds(own, 4)], gbuf.at[gn, pl.ds(own, 4)], AGA, p2).start()
 
         @pl.when(do_ag)
         def _():
@@ -325,7 +366,7 @@
 
         @pl.when(do_c)
         def _():
-            lax.fori_loop(T_OUT // 2, T_OUT, out_tile, 0)
+            lax.fori_loop(OUT_SPLIT, T_OUT, out_tile, 0)
             send_half(T_OUT - 1)
 
         @pl.when(do_ag)
@@ -344,16 +385,20 @@
     pltpu.make_async_copy(vbuf, vo_hbm.at[0, pl.ds(0, GROUP)], cosem.at[1]).wait()
 
 
+def rotary_tables():
+    lane = np.arange(128)
+    inv_freq = np.float32(1) / np.power(np.float32(10000), (lane // 2 * 2).astype(np.float32) / np.float32(ROT_DIM))
+    inv_freq = np.where(lane < ROT_DIM, inv_freq, 0).astype(np.float32)
+    angles = np.arange(SLOTS, dtype=np.float32)[:, None] * inv_freq[None, :]
+    sign = np.where(lane % 2 == 0, -1.0, 1.0)
+    return np.cos(angles.astype(np.float64)).astype(np.float32), (np.sin(angles.astype(np.float64)) * sign).astype(np.float32)
+
+
 def decode_shard(x_steps, cur_len, k_cache, v_cache, ln_gain, ln_bias, w_q, w_k, w_v, w_o, w_in, b_in, w_out, b_out):
     n_layers, batch, slots, heads, dim = k_cache.shape
     f32 = jnp.float32
-    lane = jnp.arange(128)
-    inv_freq = jnp.where(lane < ROT_DIM, 1.0 / (10000.0 ** ((lane // 2 * 2).astype(f32) / ROT_DIM)), 0.0)
-    pos = (cur_len[:, None] + jnp.arange(STEPS)[None, :]).astype(f32)
-    angles = pos[:, :, None] * inv_freq
-    cos_tab = jnp.cos(angles)
-    sin_tab = jnp.sin(angles) * jnp.where(lane % 2 == 0, -1.0, 1.0)
-    flat = (n_layers, batch, slots * heads, dim)
+    cos_tab, sin_tab = rotary_tables()
+    flat = k_cache.shape
     bf = jnp.bfloat16
     any_spec, vmem = pl.BlockSpec(memory_space=pl.ANY), pl.BlockSpec(memory_space=pltpu.VMEM)
     out, k_out, v_out = pl.pallas_call(
@@ -373,8 +418,12 @@
             pltpu.VMEM((4, ROWS, 128), f32),
             pltpu.VMEM((ROWS, ATT + FF), bf),
             pltpu.VMEM((NBUF, WIDTH, TILE), bf),
-            pltpu.VMEM((GROUP, 2 * SLOTS, HEAD), bf),
-            pltpu.VMEM((GROUP, 2 * SLOTS, HEAD), bf),
+            pltpu.VMEM((GROUP, SLOTS, HEADS, HEAD), bf),
+            pltpu.VMEM((GROUP, SLOTS, HEADS, HEAD), bf),
+            pltpu.VMEM((N_LAYERS, 1, WIDTH), f32),
+            pltpu.VMEM((N_LAYERS, 1, WIDTH), f32),
+            pltpu.VMEM((N_LAYERS, 1, WIDTH), f32),
+            pltpu.VMEM((N_LAYERS, T_IN, 1, TILE), f32),
             pltpu.SemaphoreType.DMA((NBUF,)),
             pltpu.SemaphoreType.DMA((2,)),
             pltpu.SemaphoreType.DMA((2,)),
@@ -385,11 +434,11 @@
             pltpu.SemaphoreType.DMA((6,)),
             pltpu.SemaphoreType.REGULAR((3,)),
             pltpu.SemaphoreType.REGULAR,
+            pltpu.SemaphoreType.REGULAR,
         ],
         compiler_params=pltpu.CompilerParams(collective_id=0, has_side_effects=True, vmem_limit_bytes=62 * 1024 * 1024),
     )(cur_len, x_steps, k_cache.reshape(flat), v_cache.reshape(flat),
-      ln_gain.astype(f32)[:, None], ln_bias.astype(f32)[:, None], b_out.astype(f32)[:, None],
-      b_in.astype(f32).reshape(n_layers, T_IN, 1, TILE), cos_tab, sin_tab, w_q, w_k, w_v, w_o, w_in, w_out)
+      ln_gain, ln_bias, b_out, b_in, cos_tab, sin_tab, w_q, w_k, w_v, w_o, w_in, w_out)
     return out, k_out.reshape(k_cache.shape), v_out.reshape(v_cache.shape)
 
 

time: 591 us -> 409 us (0.69)
  Pallas kernels: 510 us -> 384 us
  local copies, waits for them, and re-layouts: 71.6 us -> 24.4 us
  other arithmetic: 6.26 us -> 0 us
    pallas_call x1, Pallas kernels: 510 us -> 384 us  [decode_shard(): pl.pallas_call(kernel, out_shape=(jax.ShapeDtypeStruct(x_steps.shape, bf)...]
    reshape x5 -> x0, local copies, waits for them, and re-layouts: 53.5 us -> none  [the longest x2 26.1 us: decode_shard(): return (out, k_out.reshape(k_cache.shape), v_out.reshape(v_cache.shape))]
    unnamed x1 -> x7, local copies, waits for them, and re-layouts: 14.1 us -> 24.4 us
where the time goes in v3:
time: 409 us
  Pallas kernels  384 us (94%)
  local copies, waits for them, and re-layouts  24.4 us (6%)
    pallas_call x1, Pallas kernels, decode_shard(): pl.pallas_call(kernel, out_shape=(jax.ShapeDtypeStruct(x_steps.shape, bf)...  384 us
    unnamed x7, local copies, waits for them, and re-layouts  24.4 us

profile of v3, /device:TPU:0, one launch (start us, length us, event | category | flops | bytes accessed | tf_op | source)
XLA Modules:
  0.0 409.1 jit_solution(4646170229760284431)
XLA Ops:
  0.6 384.0 %shard_map.175 = (bf16[32,64,4096]{2,1,0:T(8,128)(2,1)}, bf16[2,64,64,2,256]{4,3,2,1,0:T(2,128)(2,1)}, bf16[2,64,64,2,256]{4,3,2,1,0:T(2,128)(2,1)}) custom-call(s32[64]{0:T(128)} %cur_ref.1, bf16[32,64,4096]{2,1,0:T(8,128)(2,1)} %x_hbm.1, bf16[2,64,64,2,256]{4,3,2,1,0:T(2,128)(2,1)} %kc_hbm.1, bf16[2,64,64,2,256]{4,3,2,1,0:T(2,128)(2,1)} %vc_hbm.1, ...), custom_call_target="tpu_custom_call" | custom-call | tf_op jit(solution)/shard_map/pallas_call | solution.py:404
  384.6 0.0 copy-start.1
  384.6 14.6 %copy.22 = bf16[32,64,4096]{2,1,0:T(8,128)(2,1)} copy(bf16[32,64,4096]{2,1,0:T(8,128)(2,1)} %get-tuple-element.6) | data formatting | bytes 33554432
  399.2 0.0 copy-done.1
  399.2 0.0 copy-start
  399.3 4.3 %copy.23 = bf16[2,64,64,2,256]{4,3,2,1,0:T(2,128)(2,1)} copy(bf16[2,64,64,2,256]{4,3,2,1,0:T(2,128)(2,1)S(1)} %copy-done.1) | data formatting | bytes 16777216
  403.5 2.2 copy-done
  405.7 3.4 copy.24
Async XLA Ops:
  384.6 14.6 %copy-start.1 = (bf16[2,64,64,2,256]{4,3,2,1,0:T(2,128)(2,1)S(1)}, bf16[2,64,64,2,256]{4,3,2,1,0:T(2,128)(2,1)}, u32[]{:S(2)}) copy-start(bf16[2,64,64,2,256]{4,3,2,1,0:T(2,128)(2,1)} %get-tuple-element.7) | copy-start | bytes 25165828
  399.2 6.4 %copy-start = (bf16[2,64,64,2,256]{4,3,2,1,0:T(2,128)(2,1)S(1)}, bf16[2,64,64,2,256]{4,3,2,1,0:T(2,128)(2,1)}, u32[]{:S(2)}) copy-start(bf16[2,64,64,2,256]{4,3,2,1,0:T(2,128)(2,1)} %get-tuple-element.8) | copy-start | bytes 25165828

commit v4 on v3

--- a/solution.py
+++ b/solution.py
@@ -23,9 +23,11 @@
 T_ALL = T_QKV + T_IN + T_OUT
 NBUF = 3
 LN_STEP = 4
-AT_STEP = 4
-TOP_TILES, OUT_SPLIT = 1, 6
-RS0, RS1, RS2, AGA, AGB, AGC = range(6)
+AT_STEP = 8
+TOP_TILES, IN_SPLIT, OUT_SPLIT = 1, 3, 4
+T_EARLY = 6
+EARLY = T_EARLY * TILE
+RS0, RS0_LATE, RS1, RS1_LATE, RS2, AGA, AGB, AGC = range(8)
 
 
 def norm_rows(x, gain, bias):
@@ -38,7 +40,7 @@
 def kernel(cur_ref, x_hbm, kc_hbm, vc_hbm, gain_in, bias_in, bout_in, bin_in, cos_ref, sin_ref,
            wq, wk, wv, wo, win, wout, out_hbm, ko_hbm, vo_hbm,
            hbuf, gbuf, pbuf, r0, r1, r2, xres, qkv, ctx, act, wbuf, kbuf, vbuf, gain_ref, bias_ref, bout_ref, bin_ref,
-           wsem, hsem, csem, cosem, xsem, gsem, ssem, rsem, ready, r0free, gfree):
+           wsem, hsem, csem, cosem, xsem, gsem, ssem, rsem, ready, gfree):
     me = lax.axis_index("tp")
     core = me % 2
     xc = (me // 2) % 2
@@ -102,11 +104,24 @@
         def _():
             pltpu.make_async_copy(out_hbm.at[:, cols, :], hbuf.at[b], hsem.at[b]).start()
 
-    def add_rows(p, base, r_ref, rbase, n):
+    def add_rows(p, base, terms, n, cols):
         def body(t, _):
-            pbuf[p, base + t] = (pbuf[p, base + t].astype(jnp.float32) + r_ref[rbase + t].astype(jnp.float32)).astype(jnp.bfloat16)
+            for k in range(2):
+                total = pbuf[p, base + 2 * t + k, :, cols].astype(jnp.float32)
+                for ref, start in terms:
+                    total = total + ref[start + 2 * t + k, :, cols].astype(jnp.float32)
+                pbuf[p, base + 2 * t + k, :, cols] = total.astype(jnp.bfloat16)
             return 0
-        lax.fori_loop(0, n, body, 0)
+        lax.fori_loop(0, n // 2, body, 0)
+
+    early, late = pl.ds(0, EARLY), pl.ds(EARLY, WIDTH - EARLY)
+    away1 = half + 8 * (1 - a1)
+    away2 = quarter + 4 * (1 - a2)
+
+    def start_exchange(p, cols, idx0, idx1):
+        remote(pbuf.at[p, pl.ds(16 - half, 16), :, cols], r0.at[p, :, :, cols], idx0, sib).wait()
+        add_rows(p, away1, [(r0.at[p], 8 * (1 - a1))], 8, cols)
+        remote(pbuf.at[p, pl.ds(away1, 8), :, cols], r1.at[:, :, cols], idx1, p1).start()
 
     for u in range(NBUF):
         issue(u)
@@ -177,29 +192,16 @@
 
         @pl.when(do_rs)
         def _():
-            remote(pbuf.at[po, pl.ds(16 - half, 16)], r0, RS0, sib).wait()
-            add_rows(po, half + 8 * (1 - a1), r0, 8 * (1 - a1), 8)
+            start_exchange(po, late, RS0_LATE, RS1_LATE)
 
         @pl.when(s >= 1)
         def _():
-            pl.semaphore_wait(ready.at[1], 1)
-
-        @pl.when(do_rs)
-        def _():
-            remote(pbuf.at[po, pl.ds(half + 8 * (1 - a1), 8)], r1, RS1, p1).start()
+            pl.semaphore_signal(ready.at[0], inc=1, device_id={"tp": sib}, device_id_type=MESH)
 
         @pl.when(do_ag)
         def _():
             remote(gbuf.at[gb, pl.ds(own, 4)], gbuf.at[gb, pl.ds(own, 4)], AGA, p2).wait()
             remote(gbuf.at[gb, pl.ds(quarter, 8)], gbuf.at[gb, pl.ds(quarter, 8)], AGB, p1).start()
-
-        @pl.when(do_rs)
-        def _():
-            add_rows(po, quarter, r0, 8 * a1, 8)
-
-        @pl.when((s >= 1) & (s < N_TASKS))
-        def _():
-            pl.semaphore_signal(r0free, inc=1, device_id={"tp": sib}, device_id_type=MESH)
 
         @pl.when(do_c)
         def _():
@@ -229,21 +231,22 @@
 
         @pl.when(do_c)
         def _():
-            lax.fori_loop(0, T_IN, in_tile, 0)
+            lax.fori_loop(0, IN_SPLIT, in_tile, 0)
+
+        @pl.when(s >= 1)
+        def _():
+            pl.semaphore_wait(ready.at[2], 1)
 
         @pl.when(do_rs)
         def _():
-            remote(pbuf.at[po, pl.ds(half + 8 * (1 - a1), 8)], r1, RS1, p1).wait()
-            add_rows(po, quarter + 4 * (1 - a2), r1, 4 * (1 - a2), 4)
-
-        @pl.when(s >= 1)
-        def _():
-            pl.semaphore_wait(ready.at[2], 1)
-
-        @pl.when(do_rs)
-        def _():
-            remote(pbuf.at[po, pl.ds(quarter + 4 * (1 - a2), 4)], r2, RS2, p2).start()
-            add_rows(po, own, r1, 4 * a2, 4)
+            for cols, idx in ((early, RS1), (late, RS1_LATE)):
+                remote(pbuf.at[po, pl.ds(away1, 8), :, cols], r1.at[:, :, cols], idx, p1).wait()
+            add_rows(po, away2, [(r0.at[po], 8 * a1 + 4 * (1 - a2)), (r1, 4 * (1 - a2))], 4, pl.ds(0, WIDTH))
+            remote(pbuf.at[po, pl.ds(away2, 4)], r2, RS2, p2).start()
+
+        @pl.when(do_c)
+        def _():
+            lax.fori_loop(IN_SPLIT, T_IN, in_tile, 0)
 
         def attend(step, _):
             seqs = [AT_STEP * step + k for k in range(AT_STEP)]
@@ -304,7 +307,7 @@
 
         def send_half(j):
             cols = pl.ds(pl.multiple_of(j * TILE, TILE), TILE)
-            remote(pbuf.at[pn, pl.ds(16 - half, 16), :, cols], r0.at[:, :, cols], RS0, sib).start()
+            remote(pbuf.at[pn, pl.ds(16 - half, 16), :, cols], r0.at[pn, :, :, cols], RS0 + j // T_EARLY, sib).start()
 
         @pl.when(do_c)
         def _():
@@ -316,21 +319,25 @@
             for k in range(4):
                 act[:, k * 128:(k + 1) * 128] = ctx[k].astype(jnp.bfloat16)
 
-            @pl.when(s >= 1)
-            def _():
-                pl.semaphore_wait(r0free, 1)
+        @pl.when(s >= 1)
+        def _():
+            pl.semaphore_wait(ready.at[0], 1)
+
+        @pl.when(do_c)
+        def _():
             lax.fori_loop(0, OUT_SPLIT, out_tile, 0)
 
         @pl.when(do_rs)
         def _():
-            remote(pbuf.at[po, pl.ds(quarter + 4 * (1 - a2), 4)], r2, RS2, p2).wait()
+            remote(pbuf.at[po, pl.ds(away2, 4)], r2, RS2, p2).wait()
 
             @pl.when(l1 == 0)
             def _():
                 pltpu.make_async_copy(x_hbm.at[pl.ds(0, 4), pl.ds(0, GROUP), :], xres.at[c1], xsem).wait()
 
             def finish(t, _):
-                tot = pbuf[po, own + t].astype(jnp.float32) + r2[t].astype(jnp.float32)
+                tot = pbuf[po, own + t].astype(jnp.float32) + r0[po, 8 * a1 + 4 * a2 + t].astype(jnp.float32)
+                tot = tot + r1[4 * a2 + t].astype(jnp.float32) + r2[t].astype(jnp.float32)
                 new = (xres[c1, t].astype(jnp.float32) + tot + bout_ref[l1]).astype(jnp.bfloat16)
 
                 @pl.when(l1 == 0)
@@ -356,10 +363,6 @@
             for k in (1, 2):
                 pl.semaphore_signal(ready.at[k], inc=1, device_id={"tp": partners[k]}, device_id_type=MESH)
 
-        @pl.when(s >= 1)
-        def _():
-            pl.semaphore_wait(ready.at[0], 1)
-
         @pl.when(do_ag)
         def _():
             remote(gbuf.at[gb, pl.ds(half, 16)], gbuf.at[gb, pl.ds(half, 16)], AGC, sib).start()
@@ -369,14 +372,18 @@
             lax.fori_loop(OUT_SPLIT, T_OUT, out_tile, 0)
             send_half(T_OUT - 1)
 
+        @pl.when(s <= N_TASKS)
+        def _():
+            pl.semaphore_wait(ready.at[1], 1)
+
+        @pl.when(do_c)
+        def _():
+            start_exchange(pn, early, RS0, RS1)
+
         @pl.when(do_ag)
         def _():
             remote(gbuf.at[gb, pl.ds(half, 16)], gbuf.at[gb, pl.ds(half, 16)], AGC, sib).wait()
             pltpu.make_async_copy(gbuf.at[gb], out_hbm.at[:, pl.ds(pl.multiple_of(c2 * GROUP, GROUP), GROUP), :], gsem).start()
-
-        @pl.when(s <= N_TASKS)
-        def _():
-            pl.semaphore_signal(ready.at[0], inc=1, device_id={"tp": sib}, device_id_type=MESH)
         return 0
 
     lax.fori_loop(0, N_TASKS + 2, slot, 0)
@@ -410,7 +417,7 @@
             pltpu.VMEM((2, STEPS, GROUP, WIDTH), bf),
             pltpu.VMEM((2, STEPS, GROUP, WIDTH), bf),
             pltpu.VMEM((2, STEPS, GROUP, WIDTH), bf),
-            pltpu.VMEM((16, GROUP, WIDTH), bf),
+            pltpu.VMEM((2, 16, GROUP, WIDTH), bf),
             pltpu.VMEM((8, GROUP, WIDTH), bf),
             pltpu.VMEM((4, GROUP, WIDTH), bf),
             pltpu.VMEM((N_GROUPS, 4, GROUP, WIDTH), bf),
@@ -430,10 +437,9 @@
             pltpu.SemaphoreType.DMA((2,)),
             pltpu.SemaphoreType.DMA,
             pltpu.SemaphoreType.DMA,
-            pltpu.SemaphoreType.DMA((6,)),
-            pltpu.SemaphoreType.DMA((6,)),
+            pltpu.SemaphoreType.DMA((8,)),
+            pltpu.SemaphoreType.DMA((8,)),
             pltpu.SemaphoreType.REGULAR((3,)),
-            pltpu.SemaphoreType.REGULAR,
             pltpu.SemaphoreType.REGULAR,
         ],
         compiler_params=pltpu.CompilerParams(collective_id=0, has_side_effects=True, vmem_limit_bytes=62 * 1024 * 1024),

time: 409 us -> 398 us (0.973)
  Pallas kernels: 384 us -> 373 us
    pallas_call x1, Pallas kernels: 384 us -> 373 us  [decode_shard(): pl.pallas_call(kernel, out_shape=(jax.ShapeDtypeStruct(x_steps.shape, bf)...]
where the time goes in v4:
time: 398 us
  Pallas kernels  373 us (94%)
  local copies, waits for them, and re-layouts  24.4 us (6%)
    pallas_call x1, Pallas kernels, decode_shard(): pl.pallas_call(kernel, out_shape=(jax.ShapeDtypeStruct(x_steps.shape, bf)...  373 us
    unnamed x7, local copies, waits for them, and re-layouts  24.4 us

profile of v4, /device:TPU:0, one launch (start us, length us, event | category | flops | bytes accessed | tf_op | source)
XLA Modules:
  0.0 398.2 jit_solution(18373962495547288084)
XLA Ops:
  0.6 373.2 %shard_map.175 = (bf16[32,64,4096]{2,1,0:T(8,128)(2,1)}, bf16[2,64,64,2,256]{4,3,2,1,0:T(2,128)(2,1)}, bf16[2,64,64,2,256]{4,3,2,1,0:T(2,128)(2,1)}) custom-call(s32[64]{0:T(128)} %cur_ref.1, bf16[32,64,4096]{2,1,0:T(8,128)(2,1)} %x_hbm.1, bf16[2,64,64,2,256]{4,3,2,1,0:T(2,128)(2,1)} %kc_hbm.1, bf16[2,64,64,2,256]{4,3,2,1,0:T(2,128)(2,1)} %vc_hbm.1, ...), custom_call_target="tpu_custom_call" | custom-call | tf_op jit(solution)/shard_map/pallas_call | solution.py:411
  373.8 0.0 copy-start.1
  373.8 14.6 %copy.22 = bf16[32,64,4096]{2,1,0:T(8,128)(2,1)} copy(bf16[32,64,4096]{2,1,0:T(8,128)(2,1)} %get-tuple-element.6) | data formatting | bytes 33554432
  388.4 0.0 copy-done.1
  388.4 0.0 copy-start
  388.4 4.3 %copy.23 = bf16[2,64,64,2,256]{4,3,2,1,0:T(2,128)(2,1)} copy(bf16[2,64,64,2,256]{4,3,2,1,0:T(2,128)(2,1)S(1)} %copy-done.1) | data formatting | bytes 16777216
  392.7 2.2 copy-done
  394.8 3.4 copy.24
Async XLA Ops:
  373.8 14.6 %copy-start.1 = (bf16[2,64,64,2,256]{4,3,2,1,0:T(2,128)(2,1)S(1)}, bf16[2,64,64,2,256]{4,3,2,1,0:T(2,128)(2,1)}, u32[]{:S(2)}) copy-start(bf16[2,64,64,2,256]{4,3,2,1,0:T(2,128)(2,1)} %get-tuple-element.7) | copy-start | bytes 25165828
  388.4 6.4 %copy-start = (bf16[2,64,64,2,256]{4,3,2,1,0:T(2,128)(2,1)S(1)}, bf16[2,64,64,2,256]{4,3,2,1,0:T(2,128)(2,1)}, u32[]{:S(2)}) copy-start(bf16[2,64,64,2,256]{4,3,2,1,0:T(2,128)(2,1)} %get-tuple-element.8) | copy-start | bytes 25165828
